TPU v7x, 16 devices: a whole 2x2x2 slice. The times are simulated.
16 devices in a mesh: data: 4 (over z, y), expert: 4 (over x, core).
Axes of the slice: x: 2, y: 2, z: 2, core: 2. Of those that a mesh axis runs over, the one named last changes fastest.
Arguments:
- x: bfloat16 [4096, 2048], P(('data', 'expert')), parts along dimension 0
- idx: int32 [4096, 5], P(('data', 'expert')), parts along dimension 0
- g: float32 [4096, 5], P(('data', 'expert')), parts along dimension 0
- hot_tok: int32 [4096], P(('data', 'expert')), parts along dimension 0
- hot_g: float32 [4096], P(('data', 'expert')), parts along dimension 0
- ln1: float32 [2048], replicated
- wq: bfloat16 [2048, 16, 128], replicated
- wk: bfloat16 [2048, 16, 128], replicated
- wv: bfloat16 [2048, 16, 128], replicated
- wo: bfloat16 [16, 128, 2048], replicated
- ln2: float32 [2048], replicated
- w1: bfloat16 [64, 2048, 1408], P('expert')
- w3: bfloat16 [64, 2048, 1408], P('expert')
- w2: bfloat16 [64, 1408, 2048], P('expert')
Outputs:
- output: bfloat16 [4096, 2048], P(('data', 'expert')), parts along dimension 0
There are 4 independent parts. A program takes and returns all parts, laid end to end along the dimension named above; an argument that names none is the same for every part.
All inputs are finite; a program needn't handle non-finite values.
Results may differ from a plain program's by a relative error of at most 0.0105217.
Values are sent between devices in bfloat16 or wider.
A program may use at most 1.25 GiB of HBM per device.

v0:
```python
import jax
import jax.numpy as jnp
from jax import lax
from jax.sharding import PartitionSpec as P

EPS = 1e-6
ROPE_BASE = 10000.0
HOT_ID = 1
F32 = jnp.float32
BF16 = jnp.bfloat16


def _rms(v, w):
    v = v.astype(F32)
    return (v * lax.rsqrt(jnp.mean(v * v, axis=-1, keepdims=True) + EPS) * w).astype(BF16)


def _rope(t):
    n_tok, _, dh = t.shape
    half = dh // 2
    freq = ROPE_BASE ** (-jnp.arange(half, dtype=F32) / half)
    ang = jnp.arange(n_tok, dtype=F32)[:, None] * freq[None, :]
    cos = jnp.cos(ang)[:, None, :]
    sin = jnp.sin(ang)[:, None, :]
    t1, t2 = t[..., :half], t[..., half:]
    return jnp.concatenate([t1 * cos - t2 * sin, t2 * cos + t1 * sin], axis=-1)


def _attention(x, ln1, wq, wk, wv, wo):
    n_tok = x.shape[0]
    dh = wq.shape[2]
    a = _rms(x, ln1)
    q = _rope(jnp.einsum('td,dhk->thk', a, wq, preferred_element_type=F32)).astype(BF16)
    k = _rope(jnp.einsum('td,dhk->thk', a, wk, preferred_element_type=F32)).astype(BF16)
    v = jnp.einsum('td,dhk->thk', a, wv, preferred_element_type=F32).astype(BF16)
    s = jnp.einsum('qhk,shk->hqs', q, k, preferred_element_type=F32) * dh ** -0.5
    mask = jnp.tril(jnp.ones((n_tok, n_tok), bool))
    p = jax.nn.softmax(jnp.where(mask[None], s, -jnp.inf), axis=-1).astype(BF16)
    o = jnp.einsum('hqs,shk->qhk', p, v, preferred_element_type=F32).astype(BF16)
    out = jnp.einsum('qhk,hkd->qd', o, wo, preferred_element_type=F32)
    return (x.astype(F32) + out).astype(BF16)


def _capacity(t, kc, n_exp):
    c0 = (t * kc + n_exp - 2) // (n_exp - 1)
    return 8 * ((3 * c0 + 15) // 16)


def _slots(e, n_exp, cap):
    r = e.shape[0]
    order = jnp.argsort(e, stable=True)
    counts = jnp.zeros((n_exp,), jnp.int32).at[e].add(1)
    starts = jnp.cumsum(counts) - counts
    rank = jnp.zeros((r,), jnp.int32).at[order].set(jnp.arange(r, dtype=jnp.int32) - starts[e[order]])
    return e * cap + rank


def _ffn(a, w1, w3, w2):
    h1 = jnp.dot(a, w1, preferred_element_type=F32)
    h3 = jnp.dot(a, w3, preferred_element_type=F32)
    z = (jax.nn.silu(h1) * h3).astype(BF16)
    return jnp.dot(z, w2, preferred_element_type=F32).astype(BF16)


def _experts(a, w1, w3, w2):
    h1 = jnp.einsum('erd,edf->erf', a, w1, preferred_element_type=F32)
    h3 = jnp.einsum('erd,edf->erf', a, w3, preferred_element_type=F32)
    z = (jax.nn.silu(h1) * h3).astype(BF16)
    return jnp.einsum('erf,efd->erd', z, w2, preferred_element_type=F32).astype(BF16)


def _combine(rows, g, hot_tok, hot_g, hot_out):
    t, kc = g.shape
    y = jnp.sum(g[:, :, None] * rows.reshape(t, kc, -1).astype(F32), axis=1)
    y = y.at[hot_tok].add(hot_g[:, None] * hot_out.astype(F32))
    return y.astype(BF16)


def solution(mesh):
    n = mesh.shape['expert']

    def local(x, idx, g, hot_tok, hot_g, ln1, wq, wk, wv, wo, ln2, w1, w3, w2):
        T, D = x.shape
        KC = idx.shape[1]
        el = w1.shape[0]
        E = el * n
        C = _capacity(T, KC, E)
        ch = hot_tok.shape[0]
        owner = HOT_ID // el
        lh = HOT_ID % el
        me = lax.axis_index('expert')
        u = _rms(_attention(x, ln1, wq, wk, wv, wo), ln2)
        slot = _slots(idx.reshape(-1), E, C)
        tok = jnp.arange(T * KC) // KC
        buf = jnp.zeros((E * C, D), BF16).at[slot].set(u[tok])
        recv = lax.all_to_all(buf, 'expert', 0, 0, tiled=True)
        xin = recv.reshape(n, el, C, D).transpose(1, 0, 2, 3).reshape(el, n * C, D)
        out = _experts(xin, w1, w3, w2)
        out = out.reshape(el, n, C, D).transpose(1, 0, 2, 3).reshape(E * C, D)
        back = lax.all_to_all(out, 'expert', 0, 0, tiled=True)
        rows = back[slot]
        hrows = lax.all_gather(u[hot_tok], 'expert', tiled=True)
        hout = lax.cond(me == owner,
                        lambda r: _ffn(r, w1[lh], w3[lh], w2[lh]),
                        lambda r: jnp.zeros_like(r),
                        hrows)
        hback = lax.all_to_all(hout, 'expert', 0, 0, tiled=True)
        hot_out = hback.reshape(n, ch, D)[owner]
        return _combine(rows, g, hot_tok, hot_g, hot_out)

    tk = ('data', 'expert')
    rep3 = P(None, None, None)
    exp3 = P('expert', None, None)
    return jax.shard_map(
        local, mesh=mesh,
        in_specs=(P(tk, None), P(tk, None), P(tk, None), P(tk), P(tk), P(None),
                  rep3, rep3, rep3, rep3, P(None), exp3, exp3, exp3),
        out_specs=P(tk, None), check_vma=False)
```

profile of v0, /device:TPU:0, one launch (start us, length us, event | category | flops | bytes accessed | tf_op | source)
XLA Modules:
  0.0 579.8 jit_solution(12618078150691965112)
XLA Ops:
  6.5 0.9 copy.22
  7.5 0.2 reshape.212
  7.7 9.4 %scatter_custom_fusion = s32[64]{0:T(128)S(1)} fusion(s32[1280]{0:T(1024)S(1)} %fusion.55, s32[1280]{0:T(1024)S(1)} %broadcast.316, s32[]{:T(128)} %constant.13.clone.1), kind=kCustom, calls=%fused_computation.162 | custom fusion | flops 1280 | bytes 260 | tf_op jit(solution)/shard_map/scatter-add | solution.py:52
  17.4 0.7 fusion.72
  18.1 0.7 fusion.73
  19.0 0.7 fusion.70
  19.7 0.7 fusion.71
  20.6 5.0 sort.17
  25.6 7.1 %gather_fusion = s32[1280]{0:T(1024)S(1)} fusion(s32[1280]{0:T(1024)S(1)} %reshape.211, s32[2048]{0:T(1024)S(1)} %pad_clamp_fusion.2), kind=kCustom, calls=%fused_computation | custom fusion | bytes 15360 | tf_op jit(solution)/shard_map/gather | solution.py:54
  32.7 4.3 fusion.54
  37.0 0.9 compare_reduce_fusion.56
  38.0 35.7 %select_subtract_fusion = s32[1280]{0:T(1024)S(1)} fusion(pred[1280]{0:T(1024)(128)(4,1)S(1)} %get-tuple-element.78, pred[1280]{0:T(1024)(128)(4,1)S(1)} %get-tuple-element.77, pred[1280]{0:T(1024)(128)(4,1)S(1)} %get-tuple-element.76, pred[1280]{0:T(1024)(128)(4,1)S(1)} %get-tuple-element.75, pred[1280]{0:T(1024)(128)(4,1)S(1)} %get-tuple-element.74, ...), kind=kLoop, calls=%fused_computation.150 | loop fusion | flops 74240 | bytes 83428 | tf_op jit(solution)/shard_map/sub | solution.py:54
  73.7 5.2 scatter_custom_fusion.1
  79.0 0.3 fusion.31
  79.3 12.4 %copy.25 = bf16[2048,16,128]{0,2,1:T(8,128)(2,1)} copy(bf16[2048,16,128]{2,1,0:T(8,128)(2,1)} %param.22) | data formatting | bytes 16777216 | tf_op args[6]
  91.7 12.5 %copy.26 = bf16[2048,16,128]{0,2,1:T(8,128)(2,1)} copy(bf16[2048,16,128]{2,1,0:T(8,128)(2,1)} %param.23) | data formatting | bytes 16777216 | tf_op args[7]
  104.2 6.1 %fusion.67 = f32[256,2048]{0,1:S(1)} fusion(bf16[2048,2048]{0,1:T(8,128)(2,1)} %bitcast.143, bf16[256,2048]{1,0:T(8,128)(2,1)S(1)} %copy-done.1, f32[2048]{0:T(1024)S(1)} %copy-done.9, f32[256]{0:T(256)S(1)} %add_rsqrt_fusion.1), kind=kOutput, calls=%fused_computation.168 | convolution fusion | flops 2149580800 | bytes 11543552
  110.3 2.5 fusion.65
  112.9 0.3 fusion.53
  113.2 2.4 fusion.21
  115.6 0.7 copy.42
  116.3 0.7 subtract_convert_fusion
  117.0 0.8 fusion.41
  117.8 3.1 fusion.74
  120.8 7.9 %fusion.28 = (f32[256]{0:T(256)S(1)}, bf16[256,2048]{1,0:T(8,128)(2,1)S(1)}) fusion(bf16[16,128,2048]{2,1,0:T(8,128)(2,1)} %param.25, f32[16,256,256]{1,2,0:T(8,128)} %get-tuple-element.154, f32[16,256]{1,0:T(8,128)S(1)} %get-tuple-element.153, bf16[256,16,128]{2,1,0:T(8,128)(2,1)S(1)} %copy.42, bf16[256,2048]{1,0:T(8,128)(2,1)S(1)} %copy-done.1), kind=kOutput, calls=%fused_computation.41 | convolution fusion | flops 2421686016 | bytes 15746048 | tf_op jit(solution)/shard_map/qhk,hkd->qd/dot_general | solution.py:40
  128.7 0.3 fusion.30
  129.1 35.3 %scatter_custom_fusion.2 = bf16[2048,2048]{1,0:T(8,128)(2,1)} fusion(s32[1280]{0:T(1024)S(1)} %compare_select_fusion.3, bf16[256,2048]{1,0:T(8,128)(2,1)S(1)} %fusion.30, s32[2048]{0:T(1024)S(1)} %pad_clamp_fusion.1, bf16[]{:T(256)} %constant.23.clone.1), kind=kCustom, calls=%fused_computation.27 | custom fusion | bytes 8388610 | tf_op jit(solution)/shard_map/scatter | solution.py:95
  164.4 5.7 all-to-all-start
  170.2 0.6 copy-done.6
  170.8 2.3 gather_fusion.2
  173.1 113.2 %all-to-all-done = bf16[4,512,2048]{2,1,0:T(8,128)(2,1)} async-done(((bf16[4,512,2048]{2,1,0:T(8,128)(2,1)}), bf16[4,512,2048]{2,1,0:T(8,128)(2,1)}, u32[]{:S(2)}, u32[]{:S(2)}) %all-to-all-start) | async-done | bytes 8388640 | tf_op jit(solution)/shard_map/all_to_all | solution.py:96
  286.3 8.3 %copy.29 = bf16[16,4,32,2048]{3,2,1,0:T(8,128)(2,1)} copy(bf16[16,4,32,2048]{3,2,0,1:T(8,128)(2,1)} %bitcast.77) | data formatting | bytes 16777216 | tf_op jit(solution)/shard_map/transpose | solution.py:97
  294.7 38.2 %fusion.77 = f32[16,128,1408]{2,1,0:T(8,128)} fusion(bf16[16,128,2048]{2,1,0:T(8,128)(2,1)} %bitcast.139, bf16[16,2048,1408]{2,1,0:T(8,128)(2,1)} %param.27), kind=kOutput, calls=%fused_computation.174 | convolution fusion | flops 11811160064 | bytes 112197632 | tf_op jit(solution)/shard_map/erd,edf->erf/dot_general | solution.py:66
  332.8 38.7 %multiply_convert_fusion.1.clone.4 = bf16[16,128,1408]{2,1,0:T(8,128)(2,1)} fusion(f32[16,128,1408]{2,1,0:T(8,128)} %fusion.77, bf16[16,128,2048]{2,1,0:T(8,128)(2,1)} %bitcast.140, bf16[16,2048,1408]{2,1,0:T(8,128)(2,1)} %param.28), kind=kOutput, calls=%fused_computation.23.clone.clone.clone.1 | convolution fusion | flops 11828461568 | bytes 117964800 | tf_op jit(solution)/shard_map/erd,edf->erf/dot_general | solution.py:67
  371.5 34.8 %convolution_convert_fusion = bf16[16,128,2048]{2,1,0:T(8,128)(2,1)} fusion(bf16[16,1408,2048]{2,1,0:T(8,128)(2,1)} %param.29, bf16[16,128,1408]{2,1,0:T(8,128)(2,1)} %multiply_convert_fusion.1.clone.4), kind=kOutput, calls=%fused_computation.26 | convolution fusion | flops 11815354368 | bytes 106430464 | tf_op jit(solution)/shard_map/erf,efd->erd/dot_general | solution.py:69
  406.3 8.3 %copy.30 = bf16[16,4,32,2048]{3,2,0,1:T(8,128)(2,1)} copy(bf16[16,4,32,2048]{3,2,1,0:T(8,128)(2,1)} %bitcast.136) | data formatting | bytes 16777216 | tf_op jit(solution)/shard_map/reshape | solution.py:99
  414.5 5.7 all-to-all-start.1
  420.2 34.5 %conditional.1 = (bf16[1024,2048]{1,0:T(8,128)(2,1)}) conditional(s32[]{:T(128)} %convert_element_type.73, () %tuple.11, (bf16[16,2048,1408]{2,1,0:T(8,128)(2,1)}, bf16[1024,2048]{1,0:T(8,128)(2,1)}, bf16[16,2048,1408]{2,1,0:T(8,128)(2,1)}, bf16[16,1408,2048]{2,1,0:T(8,128)(2,1)}) %tuple.12), branch_computations={%region_10.11_spmd, %region_11.12_spmd} | conditional | flops 17727488000 | bytes 41418760 | solution.py:103
  420.5 11.7 %fusion.4 = f32[1024,1408]{1,0:T(8,128)} fusion(bf16[1024,2048]{1,0:T(8,128)(2,1)} %get-tuple-element.16, bf16[16,2048,1408]{2,1,0:T(8,128)(2,1)} %get-tuple-element.17), kind=kOutput, calls=%fused_computation.12 | convolution fusion | flops 5905580032 | bytes 15728640 | tf_op jit(solution)/shard_map/cond/branch_1_fun/dot_general | solution.py:59
  432.2 22.6 %fusion.13 = bf16[1024,2048]{1,0:T(8,128)(2,1)} fusion(bf16[16,1408,2048]{2,1,0:T(8,128)(2,1)} %get-tuple-element.19, f32[1024,1408]{1,0:T(8,128)} %fusion.4, bf16[1024,2048]{1,0:T(8,128)(2,1)} %get-tuple-element.16, bf16[16,2048,1408]{2,1,0:T(8,128)(2,1)} %get-tuple-element.18), kind=kOutput, calls=%fused_computation.18 | convolution fusion | flops 11821907968 | bytes 25690112 | tf_op jit(solution)/shard_map/cond/branch_1_fun/dot_general | solution.py:62
  454.8 58.3 %all-to-all-done.1 = bf16[4,512,2048]{2,1,0:T(8,128)(2,1)} async-done(((bf16[4,512,2048]{2,1,0:T(8,128)(2,1)}), bf16[4,512,2048]{2,1,0:T(8,128)(2,1)}, u32[]{:S(2)}, u32[]{:S(2)}) %all-to-all-start.1) | async-done | bytes 8388640 | tf_op jit(solution)/shard_map/all_to_all | solution.py:100
  513.0 5.1 all-to-all-start.2
  518.3 15.3 %gather_fusion.1 = bf16[1280,2048]{1,0:T(8,128)(2,1)} fusion(bf16[2048,2048]{1,0:T(8,128)(2,1)} %bitcast.82, s32[2048]{0:T(1024)S(1)} %pad_clamp_fusion), kind=kCustom, calls=%fused_computation.2 | custom fusion | bytes 10490880 | tf_op jit(solution)/shard_map/gather | solution.py:101
  533.6 10.5 %reshape.218 = f32[256,5,2048]{2,1,0:T(8,128)} reshape(bf16[1280,2048]{1,0:T(8,128)(2,1)} %gather_fusion.1) | data formatting | bytes 15728640 | tf_op jit(solution)/shard_map/convert_element_type | solution.py:74
  544.1 9.2 %multiply_reduce_fusion = f32[256,2048]{1,0:T(8,128)S(1)} fusion(f32[256,5,2048]{2,1,0:T(8,128)} %reshape.218, f32[256,5]{1,0:T(8,128)S(1)} %copy.21), kind=kLoop, calls=%fused_computation.22 | loop fusion | flops 4718592 | bytes 12588032 | tf_op jit(solution)/shard_map/reduce_sum | solution.py:74
  553.3 12.7 %all-to-all-done.2 = bf16[4,256,2048]{2,1,0:T(8,128)(2,1)} async-done(((bf16[4,256,2048]{2,1,0:T(8,128)(2,1)}), bf16[4,256,2048]{2,1,0:T(8,128)(2,1)}, u32[]{:S(2)}, u32[]{:S(2)}) %all-to-all-start.2) | async-done | bytes 4194336 | tf_op jit(solution)/shard_map/all_to_all | solution.py:107
  566.0 5.4 scatter_custom_fusion.3
  571.4 1.1 convert_element_type.76
  (48 shorter events, 0.9 us)
Async XLA Ops:
  6.5 72.4 %copy-start.1 = (bf16[256,2048]{1,0:T(8,128)(2,1)S(1)}, bf16[256,2048]{1,0:T(8,128)(2,1)}, u32[]{:S(2)}) copy-start(bf16[256,2048]{1,0:T(8,128)(2,1)} %param.16) | copy-start | bytes 3145732
  79.0 50.1 %copy-start.2 = (s32[1280]{0:T(1024)}, s32[1280]{0:T(1024)S(1)}, u32[]{:S(2)}) copy-start(s32[1280]{0:T(1024)S(1)} %compare_select_fusion.3) | copy-start | bytes 15364
  91.7 12.5 %copy-start.9 = (f32[2048]{0:T(1024)S(1)}, f32[2048]{0:T(1024)}, u32[]{:S(2)}) copy-start(f32[2048]{0:T(1024)} %param.21) | copy-start | bytes 24580
  104.2 6.1 %copy-start = (bf16[2048,16,128]{0,2,1:T(8,128)(2,1)S(1)}, bf16[2048,16,128]{0,2,1:T(8,128)(2,1)}, u32[]{:S(2)}) copy-start(bf16[2048,16,128]{0,2,1:T(8,128)(2,1)} %copy.26) | copy-start | bytes 25165828
  104.2 9.0 %slice-start = ((s8[8388608]{0:T(1024)(128)(4,1)}), s8[4194304]{0:T(1024)(128)(4,1)S(1)}, s32[]{:S(2)}) async-start(s8[8388608]{0:T(1024)(128)(4,1)} %bitcast.147), calls=%async_computation.4 | async-start | bytes 8388608
  110.3 2.9 slice-start.1
  120.8 7.9 %copy-start.4 = (f32[2048]{0:T(1024)S(1)}, f32[2048]{0:T(1024)}, u32[]{:S(2)}) copy-start(f32[2048]{0:T(1024)} %param.26) | copy-start | bytes 24580
  164.4 5.7 copy-start.8
  164.4 121.9 %all-to-all-start = ((bf16[4,512,2048]{2,1,0:T(8,128)(2,1)}), bf16[4,512,2048]{2,1,0:T(8,128)(2,1)}, u32[]{:S(2)}, u32[]{:S(2)}) async-start(bf16[4,512,2048]{2,1,0:T(8,128)(2,1)} %bitcast.138), calls=%async_computation | async-start | bytes 16777216 | tf_op jit(solution)/shard_map/all_to_all | solution.py:96
  170.1 250.1 %all-gather.3.cloned.1.call-start = ((), (), s32[]{:S(2)}) async-start(), calls=%async_computation.3 | async-start | bytes 5242880 | tf_op jit(solution)/shard_map/all_gather | solution.py:102
  170.2 0.6 copy-start.6
  414.5 98.5 %all-to-all-start.1 = ((bf16[4,512,2048]{2,1,0:T(8,128)(2,1)}), bf16[4,512,2048]{2,1,0:T(8,128)(2,1)}, u32[]{:S(2)}, u32[]{:S(2)}) async-start(bf16[4,512,2048]{2,1,0:T(8,128)(2,1)} %bitcast.137), calls=%async_computation.1 | async-start | bytes 16777216 | tf_op jit(solution)/shard_map/all_to_all | solution.py:100
  454.8 63.4 %copy-start.5 = (f32[256,5]{0,1:T(8,128)S(1)}, f32[256,5]{0,1:T(8,128)}, u32[]{:S(2)}) copy-start(f32[256,5]{0,1:T(8,128)} %param.18) | copy-start | bytes 15364
  454.8 63.6 %copy-start.3 = (s32[1280]{0:T(1024)S(1)}, s32[1280]{0:T(1024)}, u32[]{:S(2)}) copy-start(s32[1280]{0:T(1024)} %copy-done.2) | copy-start | bytes 15364
  513.0 53.0 %all-to-all-start.2 = ((bf16[4,256,2048]{2,1,0:T(8,128)(2,1)}), bf16[4,256,2048]{2,1,0:T(8,128)(2,1)}, u32[]{:S(2)}, u32[]{:S(2)}) async-start(bf16[4,256,2048]{2,1,0:T(8,128)(2,1)} %bitcast.141), calls=%async_computation.2 | async-start | bytes 8388608 | tf_op jit(solution)/shard_map/all_to_all | solution.py:107
  544.1 21.9 %copy-start.7 = (f32[256]{0:T(256)S(1)}, f32[256]{0:T(256)}, u32[]{:S(2)}) copy-start(f32[256]{0:T(256)} %param.20) | copy-start | bytes 3076
Sparse Core Ops, SparseCore 0:
  173.2 58.4 all-gather.2
where the time goes:
time: 587 us; the launch traced here: 580 us
  waiting for transfers between devices  184 us (31%)
  matrix products  166 us (28%)
  local copies, waits for them, and re-layouts  123 us (21%)
  other arithmetic  76.1 us (13%)
  starting transfers between devices  16.5 us (3%)
  between operations  14.3 us (2%)
    all_to_all x1, waiting for transfers between devices, local(): recv = lax.all_to_all(buf, 'expert', 0, 0, tiled=True)  113 us
    all_to_all x1, waiting for transfers between devices, local(): back = lax.all_to_all(out, 'expert', 0, 0, tiled=True)  58.3 us
    dot_general x1, matrix products, _experts(): h3 = jnp.einsum('erd,edf->erf', a, w3, preferred_element_type=F32)  38.7 us
    dot_general x1, matrix products, _experts(): h1 = jnp.einsum('erd,edf->erf', a, w1, preferred_element_type=F32)  38.2 us
    sub x1, other arithmetic, _slots(): jnp.arange(r, dtype=jnp.int32) - starts[e[order]]  35.7 us
    scatter x1, local copies, waits for them, and re-layouts, local(): buf = jnp.zeros((E * C, D), BF16).at[slot].set(u[tok])  35.3 us
    dot_general x1, matrix products, _experts(): jnp.einsum('erf,efd->erd', z, w2, preferred_element_type=F32).astype(BF16)  34.8 us
    unnamed x28, local copies, waits for them, and re-layouts  26.6 us
  transfers between devices with their start and end apart: 4, of which 3 were waited for; matrix products, arithmetic and copies ran while one was open for 34% of the time, Pallas kernels for 0%

commit v1 on v0

v1 whole, which is shorter than its diff:
```python
import functools

import jax
import jax.numpy as jnp
from jax import lax
from jax.experimental import pallas as pl
from jax.experimental.pallas import tpu as pltpu
from jax.sharding import PartitionSpec as P

EPS = 1e-6
ROPE_BASE = 10000.0
HOT_ID = 1
SLOTS = 32
F32 = jnp.float32
BF16 = jnp.bfloat16
MESH = pl.DeviceIdType.MESH


def _rms(v, w):
    v = v.astype(F32)
    return (v * lax.rsqrt(jnp.mean(v * v, axis=-1, keepdims=True) + EPS) * w).astype(BF16)


def _rope(t):
    n_tok, _, dh = t.shape
    half = dh // 2
    freq = ROPE_BASE ** (-jnp.arange(half, dtype=F32) / half)
    ang = jnp.arange(n_tok, dtype=F32)[:, None] * freq[None, :]
    cos = jnp.cos(ang)[:, None, :]
    sin = jnp.sin(ang)[:, None, :]
    t1, t2 = t[..., :half], t[..., half:]
    return jnp.concatenate([t1 * cos - t2 * sin, t2 * cos + t1 * sin], axis=-1)


def _attention(x, ln1, wq, wk, wv, wo):
    n_tok = x.shape[0]
    dh = wq.shape[2]
    a = _rms(x, ln1)
    q = _rope(jnp.einsum('td,dhk->thk', a, wq, preferred_element_type=F32)).astype(BF16)
    k = _rope(jnp.einsum('td,dhk->thk', a, wk, preferred_element_type=F32)).astype(BF16)
    v = jnp.einsum('td,dhk->thk', a, wv, preferred_element_type=F32).astype(BF16)
    s = jnp.einsum('qhk,shk->hqs', q, k, preferred_element_type=F32) * dh ** -0.5
    mask = jnp.tril(jnp.ones((n_tok, n_tok), bool))
    p = jax.nn.softmax(jnp.where(mask[None], s, -jnp.inf), axis=-1).astype(BF16)
    o = jnp.einsum('hqs,shk->qhk', p, v, preferred_element_type=F32).astype(BF16)
    out = jnp.einsum('qhk,hkd->qd', o, wo, preferred_element_type=F32)
    return (x.astype(F32) + out).astype(BF16)


def _meta(idx, g, hot_tok, hot_g, n_exp):
    T, KC = idx.shape
    eq = idx[:, :, None] == jnp.arange(n_exp)[None, None, :]
    a = jnp.any(eq, axis=1).astype(BF16)
    low = jnp.tril(jnp.ones((T, T), BF16), -1)
    before = jnp.dot(low, a, preferred_element_type=F32)
    rank = jnp.sum(jnp.where(eq, before[:, None, :], 0.0), axis=-1)
    slot = idx.astype(F32) * SLOTS + rank
    hg = jnp.sum(jnp.where(hot_tok[:, None] == jnp.arange(T)[None, :], hot_g[:, None], 0.0), axis=0)
    return jnp.concatenate(
        [slot.T, jnp.full((8 - KC, T), -1.0, F32), g.T, hg[None], jnp.zeros((7 - KC, T), F32)], axis=0)


NU = 4
NW = 4
N2 = 8


def _moe_kernel(KC, CW, u_hbm, meta_hbm, w1, w3, w2, y_ref,
                u_all, meta, xs, zt, zh, wbuf, ob, cm, zhot, sdiag, ssib, scpt, own, rdiag, rsib, rcpt,
                in_sem, wsem, w2sem, um_send, um_recv, uc_send, uc_recv, uf_send, uf_recv, us_send, us_recv,
                dg_send, dg_recv, sb_send, sb_recv, cp_send, cp_recv):
    me = lax.axis_index('expert')
    core = me % 2
    sib = me + 1 - 2 * core
    cpt = (me + 2) % 4
    E, D, FF = w1.shape
    T = u_hbm.shape[0]
    R = E * SLOTS
    NC = D // CW
    RU = T // NU

    def start_w(i, src, odd):
        e = (i + HOT_ID) % E
        b = (2 * i + odd) % NW
        pltpu.make_async_copy(src.at[e], wbuf.at[b], wsem.at[b]).start()

    def wait_w(i, src, odd):
        b = (2 * i + odd) % NW
        pltpu.make_async_copy(src.at[0], wbuf.at[b], wsem.at[b]).wait()

    def w2_dst(t):
        sl = t % N2
        return wbuf.at[sl // 2, pl.ds(0, FF), pl.ds(pl.multiple_of((sl % 2) * CW, CW), CW)], w2sem.at[sl]

    def start_w2(t):
        dst, sem = w2_dst(t)
        e = (t % E + HOT_ID) % E
        c = t // E
        pltpu.make_async_copy(w2.at[e, :, pl.ds(pl.multiple_of(c * CW, CW), CW)], dst, sem).start()

    def wait_w2(t):
        dst, sem = w2_dst(t)
        pltpu.make_async_copy(w2.at[0, :, pl.ds(0, CW)], dst, sem).wait()

    cu = pltpu.make_async_copy(u_hbm, u_all.at[0], in_sem.at[0])
    cm_ = pltpu.make_async_copy(meta_hbm, meta.at[0], in_sem.at[1])
    cu.start()
    cm_.start()
    for i in range(NW // 2):
        start_w(i, w1, 0)
        start_w(i, w3, 1)

    barrier = pltpu.get_barrier_semaphore()
    for peer in (sib, cpt):
        pl.semaphore_signal(barrier, inc=1, device_id={'expert': peer}, device_id_type=MESH)
    cu.wait()
    cm_.wait()
    pl.semaphore_wait(barrier, 2)

    def remote(src, dst, ss, rs, peer):
        return pltpu.make_async_remote_copy(src_ref=src, dst_ref=dst, send_sem=ss, recv_sem=rs,
                                            device_id={'expert': peer}, device_id_type=MESH)

    m_sib = remote(meta.at[0], meta.at[1], um_send.at[0], um_recv.at[0], sib)
    m_cpt = remote(meta.at[0], meta.at[2], um_send.at[1], um_recv.at[1], cpt)
    m_fwd = remote(meta.at[2], meta.at[3], um_send.at[2], um_recv.at[2], sib)
    u_sib = remote(u_all.at[0], u_all.at[1], us_send, us_recv, sib)
    rows = [pl.ds(k * RU, RU) for k in range(NU)]
    u_cpt = [remote(u_all.at[0, r], u_all.at[2, r], uc_send.at[k], uc_recv.at[k], cpt) for k, r in enumerate(rows)]
    u_fwd = [remote(u_all.at[2, r], u_all.at[3, r], uf_send.at[k], uf_recv.at[k], sib) for k, r in enumerate(rows)]
    m_cpt.start()
    for c in u_cpt:
        c.start()
    m_sib.start()
    u_sib.start()

    base = (me * R).astype(F32)

    def dispatch(s):
        mt = meta[s]
        slot_iota = lax.broadcasted_iota(jnp.int32, (R, T), 0).astype(F32)
        hit = slot_iota == (mt[0:1, :] - base)
        for j in range(1, KC):
            hit = jnp.logical_or(hit, slot_iota == (mt[j:j + 1, :] - base))
        sel = jnp.where(hit, 1.0, 0.0).astype(BF16)
        for c in range(D // 512):
            cs = slice(c * 512, c * 512 + 512)
            part = jnp.dot(sel, u_all[s, :, cs], preferred_element_type=F32).astype(BF16)
            xs[:, s * SLOTS:(s + 1) * SLOTS, cs] = part.reshape(E, SLOTS, 512)
        mc = mt.T
        lane = lax.broadcasted_iota(jnp.int32, (T, R), 1).astype(F32)
        gate = jnp.zeros((T, R), F32)
        for j in range(KC):
            gate = gate + jnp.where(lane == (mc[:, j:j + 1] - base), mc[:, 8 + j:9 + j], 0.0)
        hi = gate.astype(BF16)
        r1 = gate - hi.astype(F32)
        mid = r1.astype(BF16)
        lo = (r1 - mid.astype(F32)).astype(BF16)
        cm[s, 0:T, :] = hi
        cm[s, T:2 * T, :] = mid
        cm[s, 2 * T:3 * T, :] = lo

    cols = [(0, 512), (512, 512), (1024, FF - 1024)]

    def hot_up(lo_):
        for half in range(2):
            s = lo_ + half
            for c0, cn in cols:
                a = u_all[s]
                h1 = jnp.dot(a, wbuf[0, :, c0:c0 + cn], preferred_element_type=F32)
                h3 = jnp.dot(a, wbuf[1, :, c0:c0 + cn], preferred_element_type=F32)
                zh[s, :, c0:c0 + cn] = (jax.nn.silu(h1) * h3).astype(BF16)

    def cold_up(e, b):
        for c0, cn in cols:
            a = xs[e]
            h1 = jnp.dot(a, wbuf[b, :, c0:c0 + cn], preferred_element_type=F32)
            h3 = jnp.dot(a, wbuf[b + 1, :, c0:c0 + cn], preferred_element_type=F32)
            zt[:, c0:c0 + cn] = (jax.nn.silu(h1) * h3).astype(BF16)
        xs[e, :, 0:FF] = zt[...]

    dispatch(0)
    m_sib.wait_recv()
    u_sib.wait_recv()
    dispatch(1)
    wait_w(0, w1, 0)
    wait_w(0, w3, 1)

    @pl.when(me == 0)
    def _():
        hot_up(0)

    m_cpt.wait_recv()
    m_fwd.start()
    for k in range(NU):
        u_cpt[k].wait_recv()
        u_fwd[k].start()
    dispatch(2)
    m_fwd.wait_recv()
    for k in range(NU):
        u_fwd[k].wait_recv()
    dispatch(3)

    @pl.when(me == 0)
    def _():
        hot_up(2)

    @pl.when(me != 0)
    def _():
        cold_up(HOT_ID, 0)

    start_w(NW // 2, w1, 0)
    start_w(NW // 2, w3, 1)

    def up_step(i, carry):
        e = (i + HOT_ID) % E
        b = (2 * i) % NW
        wait_w(i, w1, 0)
        wait_w(i, w3, 1)
        cold_up(e, b)

        @pl.when(i < E - NW // 2)
        def _():
            start_w(i + NW // 2, w1, 0)
            start_w(i + NW // 2, w3, 1)

        @pl.when(i >= E - NW // 2)
        def _():
            for q in range(4):
                start_w2((i - (E - NW // 2)) * 4 + q)
        return carry

    lax.fori_loop(1, E, up_step, 0)

    def chunk(c, carry):
        def down(i, carry2):
            t = c * E + i
            e = (i + HOT_ID) % E
            wait_w2(t)
            sl = t % N2
            wsl = (sl // 2, pl.ds(0, FF), pl.ds(pl.multiple_of((sl % 2) * CW, CW), CW))
            hot = jnp.logical_and(i == 0, me == 0)

            @pl.when(hot)
            def _():
                for s in range(4):
                    o = jnp.dot(zh[s], wbuf[wsl], preferred_element_type=F32).astype(BF16)
                    hg = meta[s].T[:, 13:14]
                    zhot[s] = hg * o.astype(F32)
                ob[:, HOT_ID * SLOTS:(HOT_ID + 1) * SLOTS, :] = jnp.zeros((4, SLOTS, CW), BF16)

            @pl.when(jnp.logical_not(hot))
            def _():
                o = jnp.dot(xs[e, :, 0:FF], wbuf[wsl], preferred_element_type=F32).astype(BF16)
                ob[:, pl.ds(pl.multiple_of(e * SLOTS, SLOTS), SLOTS), :] = o.reshape(4, SLOTS, CW)

            @pl.when(t + N2 < NC * E)
            def _():
                start_w2(t + N2)
            return carry2

        lax.fori_loop(0, E, down, 0)

        def combine(s):
            r = jnp.dot(cm[s], ob[s], preferred_element_type=F32)
            return (r[0:T] + r[T:2 * T]) + r[2 * T:3 * T] + zhot[s]

        p = c % 2
        d_cp = remote(sdiag.at[p], rdiag.at[c], dg_send.at[p], dg_recv.at[c], sib)
        s_cp = remote(ssib.at[p], rsib.at[c], sb_send.at[p], sb_recv.at[c], sib)
        x_cp = remote(scpt.at[c], rcpt.at[c], cp_send.at[c], cp_recv.at[c], cpt)

        @pl.when(c >= 2)
        def _():
            d_cp.wait_send()
            s_cp.wait_send()

        sdiag[p] = combine(3)
        d_cp.start()
        ssib[p] = combine(1)
        s_cp.start()
        scpt[c] = combine(2)
        own[c] = combine(0)
        d_cp.wait_recv()
        scpt[c] = scpt[c] + rdiag[c]
        x_cp.start()
        return carry

    zhot[...] = jnp.zeros_like(zhot)
    lax.fori_loop(0, NC, chunk, 0)

    for c in range(NC):
        cs = slice(c * CW, c * CW + CW)
        remote(ssib.at[0], rsib.at[c], sb_send.at[0], sb_recv.at[c], sib).wait_recv()
        remote(scpt.at[c], rcpt.at[c], cp_send.at[c], cp_recv.at[c], cpt).wait_recv()
        y_ref[:, cs] = (own[c] + rsib[c] + rcpt[c]).astype(BF16)

    m_sib.wait_send()
    m_cpt.wait_send()
    m_fwd.wait_send()
    u_sib.wait_send()
    for k in range(NU):
        u_cpt[k].wait_send()
        u_fwd[k].wait_send()
    for p in range(2):
        remote(sdiag.at[p], rdiag.at[p], dg_send.at[p], dg_recv.at[p], sib).wait_send()
        remote(ssib.at[p], rsib.at[p], sb_send.at[p], sb_recv.at[p], sib).wait_send()
    for c in range(NC):
        remote(scpt.at[c], rcpt.at[c], cp_send.at[c], cp_recv.at[c], cpt).wait_send()


def _moe(u, meta, w1, w3, w2, KC):
    T, D = u.shape
    E, _, FF = w1.shape
    CW = 512
    NC = D // CW
    R = E * SLOTS
    dma = pltpu.SemaphoreType.DMA
    any_spec = pl.BlockSpec(memory_space=pl.ANY)
    part = pltpu.VMEM((NC, T, CW), F32)
    flops = 6 * D * FF * (E * 4 * SLOTS + T)
    return pl.pallas_call(
        functools.partial(_moe_kernel, KC, CW),
        out_shape=jax.ShapeDtypeStruct((T, D), BF16),
        in_specs=[any_spec] * 5,
        out_specs=pl.BlockSpec(memory_space=pltpu.VMEM),
        scratch_shapes=[
            pltpu.VMEM((4, T, D), BF16),
            pltpu.VMEM((4, 16, T), F32),
            pltpu.VMEM((E, 4 * SLOTS, D), BF16),
            pltpu.VMEM((4 * SLOTS, FF), BF16),
            pltpu.VMEM((4, T, FF), BF16),
            pltpu.VMEM((NW, D, FF), BF16),
            pltpu.VMEM((4, R, CW), BF16),
            pltpu.VMEM((4, 3 * T, R), BF16),
            pltpu.VMEM((4, T, CW), F32),
            pltpu.VMEM((2, T, CW), F32),
            pltpu.VMEM((2, T, CW), F32),
            part, part, part, part, part,
            dma((2,)), dma((NW,)), dma((N2,)),
            dma((3,)), dma((3,)),
            dma((NU,)), dma((NU,)), dma((NU,)), dma((NU,)),
            dma, dma,
            dma((2,)), dma((NC,)), dma((2,)), dma((NC,)), dma((NC,)), dma((NC,)),
        ],
        compiler_params=pltpu.CompilerParams(
            collective_id=0, has_side_effects=True, vmem_limit_bytes=67000000),
        cost_estimate=pl.CostEstimate(flops=flops, bytes_accessed=6 * E * D * FF, transcendentals=0),
        name='moe',
    )(u, meta, w1, w3, w2)


def solution(mesh):
    def local(x, idx, g, hot_tok, hot_g, ln1, wq, wk, wv, wo, ln2, w1, w3, w2):
        n_exp = w1.shape[0] * mesh.shape['expert']
        meta = _meta(idx, g, hot_tok, hot_g, n_exp)
        u = _rms(_attention(x, ln1, wq, wk, wv, wo), ln2)
        return _moe(u, meta, w1, w3, w2, idx.shape[1])

    tk = ('data', 'expert')
    rep3 = P(None, None, None)
    exp3 = P('expert', None, None)
    return jax.shard_map(
        local, mesh=mesh,
        in_specs=(P(tk, None), P(tk, None), P(tk, None), P(tk), P(tk), P(None),
                  rep3, rep3, rep3, rep3, P(None), exp3, exp3, exp3),
        out_specs=P(tk, None), check_vma=False)
```

time: 587 us -> 210 us (0.36); the launches traced: 580 us -> 209 us
  waiting for transfers between devices: 184 us -> 0 us
  Pallas kernels: 0 us -> 149 us
  matrix products: 166 us -> 22.9 us
  local copies, waits for them, and re-layouts: 123 us -> 29.9 us
  other arithmetic: 76.1 us -> 7.22 us
  starting transfers between devices: 16.5 us -> 0 us
  between operations: 14.3 us -> 0.23 us
    all_to_all x3 -> x0, waiting for transfers between devices: 184 us -> none  [the longest x1 113 us: local(): recv = lax.all_to_all(buf, 'expert', 0, 0, tiled=True)]
    pallas_call x0 -> x1, Pallas kernels: none -> 149 us  [_moe(): pl.pallas_call(functools.partial(_moe_kernel, KC, CW), out_shape=jax.Shap...]
    dot_general x5 -> x1, matrix products: 146 us -> 0.24 us  [_meta(): before = jnp.dot(low, a, preferred_element_type=F32)]
    scatter x2 -> x0, local copies, waits for them, and re-layouts: 40.6 us -> none  [the longest x1 35.3 us: local(): buf = jnp.zeros((E * C, D), BF16).at[slot].set(u[tok])]
    sub x2 -> x0, other arithmetic: 35.7 us -> none  [the longest x1 35.7 us: _slots(): jnp.arange(r, dtype=jnp.int32) - starts[e[order]]]
    gather x7 -> x0, local copies, waits for them, and re-layouts: 27.5 us -> none  [the longest x1 15.3 us: local(): rows = back[slot]]
    all_to_all x3 -> x0, starting transfers between devices: 16.5 us -> none  [the longest x1 5.66 us: local(): recv = lax.all_to_all(buf, 'expert', 0, 0, tiled=True)]
    scatter-add x2 -> x0, other arithmetic: 14.7 us -> none  [the longest x1 9.38 us: _slots(): counts = jnp.zeros((n_exp,), jnp.int32).at[e].add(1)]
  transfers between devices with their start and end apart: 4 -> 0, of which waited for: 3 -> 0; matrix products, arithmetic and copies ran while one was open for 34% -> 0% of each run, Pallas kernels for 0% -> 0%
where the time goes in v1:
time: 210 us; the launch traced here: 209 us
  Pallas kernels  149 us (71%)
  local copies, waits for them, and re-layouts  29.9 us (14%)
  matrix products  22.9 us (11%)
  other arithmetic  7.22 us (3%)
    pallas_call x1, Pallas kernels, _moe(): pl.pallas_call(functools.partial(_moe_kernel, KC, CW), out_shape=jax.Shap...  149 us
    unnamed x21, local copies, waits for them, and re-layouts  28 us
    unnamed x2, matrix products  11.7 us
    dot_general x1, matrix products, _attention(): out = jnp.einsum('qhk,hkd->qd', o, wo, preferred_element_type=F32)  7.85 us

profile of v1, /device:TPU:0, one launch (start us, length us, event | category | flops | bytes accessed | tf_op | source)
XLA Modules:
  0.0 209.3 jit_solution(18269819123916402148)
XLA Ops:
  0.0 1.5 fusion.8
  1.5 0.0 copy-start
  1.5 0.0 copy-start.6
  1.5 12.4 %copy.21 = bf16[2048,16,128]{0,2,1:T(8,128)(2,1)} copy(bf16[2048,16,128]{2,1,0:T(8,128)(2,1)} %param.20) | data formatting | bytes 16777216 | tf_op args[6]
  13.9 0.0 copy-done
  13.9 0.0 copy-done.6
  13.9 5.8 %fusion.43 = f32[256,2048]{0,1:S(1)} fusion(bf16[2048,2048]{0,1:T(8,128)(2,1)} %bitcast.27, bf16[256,2048]{1,0:T(8,128)(2,1)S(1)} %copy-done, f32[2048]{0:T(1024)S(1)} %copy-done.6, f32[256]{0:T(256)S(1)} %add_rsqrt_fusion.1), kind=kOutput, calls=%fused_computation.66 | convolution fusion | flops 2149580800 | bytes 11543552
  19.8 12.3 %copy.22 = bf16[2048,16,128]{0,2,1:T(8,128)(2,1)} copy(bf16[2048,16,128]{2,1,0:T(8,128)(2,1)} %param.21) | data formatting | bytes 16777216 | tf_op args[7]
  32.1 5.8 %fusion.41 = f32[256,2048]{0,1:S(1)} fusion(bf16[2048,2048]{0,1:T(8,128)(2,1)} %bitcast.28, bf16[256,2048]{1,0:T(8,128)(2,1)S(1)} %copy-done, f32[2048]{0:T(1024)S(1)} %copy-done.6, f32[256]{0:T(256)S(1)} %add_rsqrt_fusion.1), kind=kOutput, calls=%fused_computation.65 | convolution fusion | flops 2149580800 | bytes 11543552
  38.0 0.3 fusion.35
  38.3 0.7 subtract_convert_fusion
  39.0 0.0 slice-start
  39.0 0.8 fusion.17
  39.8 0.0 slice-start.1
  39.8 3.1 %fusion.46 = (f32[16,256]{1,0:T(8,128)S(1)}, f32[16,256,256]{1,2,0:T(8,128)}) fusion(f32[16,256,256]{1,2,0:T(8,128)S(1)} %fusion.17, pred[256,256]{0,1:T(8,128)(4,1)S(1)} %iota_compare_fusion.3), kind=kOutput, calls=%fused_computation.67 | output fusion | flops 6291711 | bytes 8470528 | tf_op jit(solution)/shard_map/sub | solution.py:44
  42.9 0.0 slice-done
  42.9 0.9 slice-done.1
  43.9 2.4 %fusion.1 = bf16[256,16,128]{2,0,1:T(8,128)(2,1)S(1)} fusion(bf16[2048,16,128]{2,1,0:T(8,128)(2,1)S(1)} %bitcast.34, bf16[256,2048]{1,0:T(8,128)(2,1)S(1)} %copy-done, f32[2048]{0:T(1024)S(1)} %copy-done.6, f32[256]{0:T(256)S(1)} %add_rsqrt_fusion.1), kind=kOutput, calls=%fused_computation.1 | convolution fusion | flops 2149580800 | bytes 10494976 | tf_op jit(solution)/shard_map/td,dhk->thk/dot_general | solution.py:41
  46.3 0.7 copy.36
  47.0 0.0 copy-start.2
  47.0 0.0 copy-start.1
  47.0 0.0 copy-start.4
  47.0 0.0 copy-start.5
  47.0 0.0 copy-start.3
  47.0 7.9 %fusion.5 = (f32[256]{0:T(256)S(1)}, bf16[256,2048]{1,0:T(8,128)(2,1)S(1)}) fusion(bf16[16,128,2048]{2,1,0:T(8,128)(2,1)} %param.23, f32[16,256,256]{1,2,0:T(8,128)} %get-tuple-element.14, f32[16,256]{1,0:T(8,128)S(1)} %get-tuple-element.13, bf16[256,16,128]{2,1,0:T(8,128)(2,1)S(1)} %copy.36, bf16[256,2048]{1,0:T(8,128)(2,1)S(1)} %copy-done), kind=kOutput, calls=%fused_computation.14 | convolution fusion | flops 2421686016 | bytes 15746048 | tf_op jit(solution)/shard_map/qhk,hkd->qd/dot_general | solution.py:46
  54.9 0.0 copy-done.2
  54.9 1.3 fusion.7.u_hbm
  56.2 0.0 copy-done.1
  56.2 0.2 fusion.29
  56.5 0.1 select_reduce_fusion
  56.6 0.0 copy-done.4
  56.6 0.0 copy-done.5
  56.6 0.1 select_reduce_fusion.1
  56.7 0.0 copy-done.3
  56.8 1.2 concatenate.13.meta_hbm
  58.0 149.0 %moe.1 = bf16[256,2048]{1,0:T(8,128)(2,1)} custom-call(bf16[256,2048]{1,0:T(8,128)(2,1)} %fusion.7.u_hbm, f32[16,256]{1,0:T(8,128)} %concatenate.13.meta_hbm, bf16[16,2048,1408]{2,1,0:T(8,128)(2,1)} %w1.1, bf16[16,2048,1408]{2,1,0:T(8,128)(2,1)} %w3.1, bf16[16,1408,2048]{2,1,0:T(8,128)(2,1)} %w2.1), custom_call_target="tpu_custom_call" | custom-call | flops 39862665216 | bytes 276824064 | tf_op jit(solution)/shard_map/moe/pallas_call | solution.py:322
  207.0 2.3 %copy.40 = bf16[256,2048]{1,0:T(8,128)(2,1)} copy(bf16[256,2048]{1,0:T(8,128)(2,1)} %moe.1) | data formatting | bytes 2097152
  (10 shorter events, 0.1 us)
Async XLA Ops:
  1.5 12.4 %copy-start = (bf16[256,2048]{1,0:T(8,128)(2,1)S(1)}, bf16[256,2048]{1,0:T(8,128)(2,1)}, u32[]{:S(2)}) copy-start(bf16[256,2048]{1,0:T(8,128)(2,1)} %param.14) | copy-start | bytes 3145732
  1.5 12.4 %copy-start.6 = (f32[2048]{0:T(1024)S(1)}, f32[2048]{0:T(1024)}, u32[]{:S(2)}) copy-start(f32[2048]{0:T(1024)} %param.19) | copy-start | bytes 24580
  39.0 4.0 %slice-start = ((s8[8388608]{0:T(1024)(128)(4,1)}), s8[4194304]{0:T(1024)(128)(4,1)S(1)}, s32[]{:S(2)}) async-start(s8[8388608]{0:T(1024)(128)(4,1)} %bitcast.33), calls=%async_computation | async-start | bytes 8388608
  39.8 4.1 %slice-start.1 = ((s8[8388608]{0:T(1024)(128)(4,1)}), s8[4194304]{0:T(1024)(128)(4,1)S(1)}, s32[]{:S(2)}) async-start(s8[8388608]{0:T(1024)(128)(4,1)} %bitcast.33), calls=%async_computation.1 | async-start | bytes 8388608
  47.0 7.9 %copy-start.2 = (f32[2048]{0:T(1024)S(1)}, f32[2048]{0:T(1024)}, u32[]{:S(2)}) copy-start(f32[2048]{0:T(1024)} %param.24) | copy-start | bytes 24580
  47.0 9.2 %copy-start.1 = (s32[256,5]{0,1:T(8,128)S(1)}, s32[256,5]{0,1:T(8,128)}, u32[]{:S(2)}) copy-start(s32[256,5]{0,1:T(8,128)} %param.15) | copy-start | bytes 15364
  47.0 9.6 %copy-start.4 = (f32[256]{0:T(256)S(1)}, f32[256]{0:T(256)}, u32[]{:S(2)}) copy-start(f32[256]{0:T(256)} %param.18) | copy-start | bytes 3076
  47.0 9.6 %copy-start.5 = (s32[256]{0:T(256)S(1)}, s32[256]{0:T(256)}, u32[]{:S(2)}) copy-start(s32[256]{0:T(256)} %param.17) | copy-start | bytes 3076
  47.0 9.7 %copy-start.3 = (f32[256,5]{0,1:T(8,128)S(1)}, f32[256,5]{0,1:T(8,128)}, u32[]{:S(2)}) copy-start(f32[256,5]{0,1:T(8,128)} %param.16) | copy-start | bytes 15364

commit v2 on v1

v2 whole, which is shorter than its diff:
```python
import functools

import jax
import jax.numpy as jnp
import numpy as np
from jax import lax
from jax.experimental import pallas as pl
from jax.experimental.pallas import tpu as pltpu
from jax.sharding import PartitionSpec as P

EPS = 1e-6
ROPE_BASE = 10000.0
HOT_ID = 1
SLOTS = 32
F32 = jnp.float32
BF16 = jnp.bfloat16
MESH = pl.DeviceIdType.MESH


def _rms(v, w):
    v = v.astype(F32)
    return (v * lax.rsqrt(jnp.mean(v * v, axis=-1, keepdims=True) + EPS) * w).astype(BF16)


def _tables(n_tok, dh):
    half = dh // 2
    freq = np.float32(ROPE_BASE) ** (-np.arange(half, dtype=np.float32) / np.float32(half))
    ang = np.arange(n_tok, dtype=np.float32)[:, None] * freq[None, :].astype(np.float32)
    cos = np.cos(ang).astype(np.float32)
    sin = np.sin(ang).astype(np.float32)
    return np.concatenate([cos, cos], axis=1), np.concatenate([-sin, sin], axis=1)


def _meta(idx, g, hot_tok, hot_g, n_exp):
    T, KC = idx.shape
    eq = idx[:, :, None] == jnp.arange(n_exp)[None, None, :]
    a = jnp.any(eq, axis=1).astype(BF16)
    low = jnp.tril(jnp.ones((T, T), BF16), -1)
    before = jnp.dot(low, a, preferred_element_type=F32)
    rank = jnp.sum(jnp.where(eq, before[:, None, :], 0.0), axis=-1)
    slot = idx.astype(F32) * SLOTS + rank
    hg = jnp.sum(jnp.where(hot_tok[:, None] == jnp.arange(T)[None, :], hot_g[:, None], 0.0), axis=0)
    return jnp.concatenate(
        [slot.T, jnp.full((8 - KC, T), -1.0, F32), g.T, hg[None], jnp.zeros((7 - KC, T), F32)], axis=0)


NU = 4
NW = 4
N2 = 8
G2 = 4


def _moe_kernel(KC, CW, q_hbm, k_hbm, v_hbm, x_hbm, wo, cos_ref, sin_ref, ln2_ref, meta_hbm, w1, w3, w2, y_ref,
                u_all, meta, xs, zt, zh, wbuf, ob, cm, sel, zhot, sdiag, ssib, scpt, own, rdiag, rsib, rcpt,
                in_sem, q_sem, k_sem, v_sem, wsem, w2sem, um_send, um_recv, uc_send, uc_recv, uf_send, uf_recv,
                us_send, us_recv, dg_send, dg_recv, sb_send, sb_recv, cp_send, cp_recv):
    me = lax.axis_index('expert')
    core = me % 2
    sib = me + 1 - 2 * core
    cpt = (me + 2) % 4
    E, D, FF = w1.shape
    NH, T, DH = q_hbm.shape
    HT = T // 2
    R = E * SLOTS
    NC = D // CW
    RU = T // NU

    def start_w(i, src, odd):
        e = (i + HOT_ID) % E
        b = (2 * i + odd) % NW
        pltpu.make_async_copy(src.at[e], wbuf.at[b], wsem.at[b]).start()

    def wait_w(i, src, odd):
        b = (2 * i + odd) % NW
        pltpu.make_async_copy(src.at[0], wbuf.at[b], wsem.at[b]).wait()

    def w2_dst(t):
        sl = t % N2
        return wbuf.at[sl // 2, pl.ds(0, FF), pl.ds(pl.multiple_of((sl % 2) * CW, CW), CW)], w2sem.at[sl]

    def start_w2(t):
        dst, sem = w2_dst(t)
        e = (t % E + HOT_ID) % E
        c = t // E
        pltpu.make_async_copy(w2.at[e, :, pl.ds(pl.multiple_of(c * CW, CW), CW)], dst, sem).start()

    def wait_w2(t):
        dst, sem = w2_dst(t)
        pltpu.make_async_copy(w2.at[0, :, pl.ds(0, CW)], dst, sem).wait()

    HB = CW // DH

    def head_copy(src, dst, sem, h):
        c, lane = h // HB, (h % HB) * DH
        return pltpu.make_async_copy(src.at[h], dst.at[c, pl.ds(0, T), pl.ds(lane, DH)], sem.at[h])

    def head_wait(src, dst, sem, c, j):
        pltpu.make_async_copy(src.at[0], dst.at[c, pl.ds(0, T), pl.ds(j * DH, DH)], sem.at[c * HB + j]).wait()

    for h in range(NH):
        head_copy(q_hbm, own, q_sem, h).start()
        head_copy(k_hbm, scpt, k_sem, h).start()
        head_copy(v_hbm, ob, v_sem, h).start()
    cx = [pltpu.make_async_copy(x_hbm.at[pl.ds(i * HT, HT)], xs.at[2 + i], in_sem.at[i]) for i in range(2)]
    cwo = [pltpu.make_async_copy(wo.at[:, pl.ds(i * D // 2, D // 2)], wbuf.at[2 + i, :, pl.ds(0, D // 2)],
                                 in_sem.at[2 + i]) for i in range(2)]
    cm_ = pltpu.make_async_copy(meta_hbm, meta.at[0], in_sem.at[4])
    for c in cx + cwo + [cm_]:
        c.start()
    start_w(0, w1, 0)
    start_w(0, w3, 1)

    barrier = pltpu.get_barrier_semaphore()
    for peer in (sib, cpt):
        pl.semaphore_signal(barrier, inc=1, device_id={'expert': peer}, device_id_type=MESH)

    def remote(src, dst, ss, rs, peer):
        return pltpu.make_async_remote_copy(src_ref=src, dst_ref=dst, send_sem=ss, recv_sem=rs,
                                            device_id={'expert': peer}, device_id_type=MESH)

    m_sib = remote(meta.at[0], meta.at[1], um_send.at[0], um_recv.at[0], sib)
    m_cpt = remote(meta.at[0], meta.at[2], um_send.at[1], um_recv.at[1], cpt)
    m_fwd = remote(meta.at[2], meta.at[3], um_send.at[2], um_recv.at[2], sib)
    u_sib = [remote(u_all.at[0, pl.ds(i * HT, HT)], u_all.at[1, pl.ds(i * HT, HT)], us_send.at[i], us_recv.at[i], sib)
             for i in range(2)]

    def u_cpt(k):
        r = pl.ds(k * RU, RU)
        return remote(u_all.at[0, r], u_all.at[2, r], uc_send.at[k], uc_recv.at[k], cpt)

    def u_fwd(k):
        r = pl.ds(k * RU, RU)
        return remote(u_all.at[2, r], u_all.at[3, r], uf_send.at[k], uf_recv.at[k], sib)

    scale = DH ** -0.5

    def attend(half):
        r0 = half * HT
        nk = r0 + HT
        cos = cos_ref[r0:nk, :]
        sin = sin_ref[r0:nk, :]

        def rope(t):
            return (t * cos + pltpu.roll(t, DH // 2, 1) * sin).astype(BF16)

        row = lax.broadcasted_iota(jnp.int32, (HT, nk), 0) + r0
        seen = row >= lax.broadcasted_iota(jnp.int32, (HT, nk), 1)

        def heads(c, carry):
            for j in range(HB):
                ls = slice(j * DH, (j + 1) * DH)
                if half == 0:
                    head_wait(q_hbm, own, q_sem, c, j)
                    head_wait(k_hbm, scpt, k_sem, c, j)
                    head_wait(v_hbm, ob, v_sem, c, j)
            for j in range(HB):
                ls = slice(j * DH, (j + 1) * DH)
                q = rope(own[c, r0:nk, ls])
                ob[c, T + r0:T + nk, ls] = rope(scpt[c, r0:nk, ls])
                s = lax.dot_general(q, ob[c, T:T + nk, ls], (((1,), (1,)), ((), ())),
                                    preferred_element_type=F32) * scale
                s = jnp.where(seen, s, -jnp.inf)
                p = jnp.exp(s - jnp.max(s, axis=1, keepdims=True))
                p = (p * (1.0 / jnp.sum(p, axis=1, keepdims=True))).astype(BF16)
                o = jnp.dot(p, ob[c, 0:nk, ls], preferred_element_type=F32)
                xs[half, :, pl.ds(pl.multiple_of(c * CW + j * DH, DH), DH)] = o.astype(BF16)
            return carry

        lax.fori_loop(0, NH // HB, heads, 0)
        cx[half].wait()
        if half == 0:
            cwo[0].wait()
            cwo[1].wait()
        ss = jnp.zeros((HT, 1), F32)
        for n in range(NC):
            cs = slice(n * CW, (n + 1) * CW)
            wn = (n * CW) // (D // 2)
            w0 = n * CW - wn * (D // 2)
            o = jnp.dot(xs[half], wbuf[2 + wn, :, w0:w0 + CW], preferred_element_type=F32)
            h = (xs[2 + half, :, cs].astype(F32) + o).astype(BF16).astype(F32)
            zhot[n, 0:HT, :] = h
            ss = ss + jnp.sum(h * h, axis=1, keepdims=True)
        inv = lax.rsqrt(ss * (1.0 / D) + EPS)
        for n in range(NC):
            cs = slice(n * CW, (n + 1) * CW)
            u_all[0, r0:nk, cs] = (zhot[n, 0:HT, :] * inv * ln2_ref[0:1, cs]).astype(BF16)

    attend(0)
    cm_.wait()
    pl.semaphore_wait(barrier, 2)
    m_cpt.start()
    for k in range(NU // 2):
        u_cpt(k).start()
    m_sib.start()
    u_sib[0].start()
    attend(1)
    for k in range(NU // 2, NU):
        u_cpt(k).start()
    u_sib[1].start()
    start_w(1, w1, 0)
    start_w(1, w3, 1)

    base = (me * R).astype(F32)

    def select(s):
        mt = meta[s]
        slot_iota = lax.broadcasted_iota(jnp.int32, (R, T), 0).astype(F32)
        hit = slot_iota == (mt[0:1, :] - base)
        for j in range(1, KC):
            hit = jnp.logical_or(hit, slot_iota == (mt[j:j + 1, :] - base))
        sel[s] = jnp.where(hit, 1.0, 0.0).astype(BF16)
        mc = mt.T
        lane = lax.broadcasted_iota(jnp.int32, (T, R), 1).astype(F32)
        gate = jnp.zeros((T, R), F32)
        for j in range(KC):
            gate = gate + jnp.where(lane == (mc[:, j:j + 1] - base), mc[:, 8 + j:9 + j], 0.0)
        hi = gate.astype(BF16)
        r1 = gate - hi.astype(F32)
        mid = r1.astype(BF16)
        lo = (r1 - mid.astype(F32)).astype(BF16)
        cm[s, 0:T, :] = hi
        cm[s, T:2 * T, :] = mid
        cm[s, 2 * T:3 * T, :] = lo

    def dispatch(s):
        for c in range(D // 512):
            cs = slice(c * 512, c * 512 + 512)
            part = jnp.dot(sel[s], u_all[s, :, cs], preferred_element_type=F32).astype(BF16)
            xs[:, s * SLOTS:(s + 1) * SLOTS, cs] = part.reshape(E, SLOTS, 512)

    cols = [(0, 512), (512, 512), (1024, FF - 1024)]

    def hot_local(s, carry):
        for c0, cn in cols:
            a = u_all[s]
            h1 = jnp.dot(a, wbuf[0, :, c0:c0 + cn], preferred_element_type=F32)
            h3 = jnp.dot(a, wbuf[1, :, c0:c0 + cn], preferred_element_type=F32)
            zh[s, :, c0:c0 + cn] = (jax.nn.silu(h1) * h3).astype(BF16)
        return carry

    def hot_batch(k):
        r = pl.ds(pl.multiple_of(k * RU, RU), RU)
        a = jnp.concatenate([u_all[2, r, :], u_all[3, r, :]], axis=0)
        for c0, cn in cols:
            h1 = jnp.dot(a, wbuf[0, :, c0:c0 + cn], preferred_element_type=F32)
            h3 = jnp.dot(a, wbuf[1, :, c0:c0 + cn], preferred_element_type=F32)
            z = (jax.nn.silu(h1) * h3).astype(BF16)
            zh[2, r, c0:c0 + cn] = z[0:RU]
            zh[3, r, c0:c0 + cn] = z[RU:]

    def cold_up(e, b):
        for c0, cn in cols:
            a = xs[e]
            h1 = jnp.dot(a, wbuf[b, :, c0:c0 + cn], preferred_element_type=F32)
            h3 = jnp.dot(a, wbuf[b + 1, :, c0:c0 + cn], preferred_element_type=F32)
            zt[:, c0:c0 + cn] = (jax.nn.silu(h1) * h3).astype(BF16)
        xs[e, :, 0:FF] = zt[...]

    select(0)
    dispatch(0)
    m_sib.wait_recv()
    select(1)
    m_cpt.wait_recv()
    m_fwd.start()
    select(2)
    for i in range(2):
        u_sib[i].wait_recv()
    dispatch(1)
    wait_w(0, w1, 0)
    wait_w(0, w3, 1)

    @pl.when(me == 0)
    def _():
        lax.fori_loop(0, 2, hot_local, 0)

    m_fwd.wait_recv()
    select(3)
    u_cpt(0).wait_recv()
    u_fwd(0).start()

    def arrive(k, carry):
        u_cpt(k).wait_recv()
        u_fwd(k).start()
        u_fwd(k - 1).wait_recv()

        @pl.when(me == 0)
        def _():
            hot_batch(k - 1)
        return carry

    lax.fori_loop(1, NU, arrive, 0)
    dispatch(2)
    u_fwd(NU - 1).wait_recv()
    dispatch(3)

    @pl.when(me == 0)
    def _():
        hot_batch(NU - 1)

    @pl.when(me != 0)
    def _():
        cold_up(HOT_ID, 0)

    start_w(NW // 2, w1, 0)
    start_w(NW // 2, w3, 1)

    def up_step(i, carry):
        e = (i + HOT_ID) % E
        b = (2 * i) % NW
        wait_w(i, w1, 0)
        wait_w(i, w3, 1)
        cold_up(e, b)

        @pl.when(i < E - NW // 2)
        def _():
            start_w(i + NW // 2, w1, 0)
            start_w(i + NW // 2, w3, 1)

        @pl.when(i >= E - NW // 2)
        def _():
            for q in range(4):
                start_w2((i - (E - NW // 2)) * 4 + q)
        return carry

    lax.fori_loop(1, E, up_step, 0)

    def chunk(c, carry):
        def slot(t):
            sl = t % N2
            return (sl // 2, pl.ds(0, FF), pl.ds(pl.multiple_of((sl % 2) * CW, CW), CW))

        def cold_down(t):
            e = (t % E + HOT_ID) % E
            o = jnp.dot(xs[e, :, 0:FF], wbuf[slot(t)], preferred_element_type=F32).astype(BF16)
            ob[:, pl.ds(pl.multiple_of(e * SLOTS, SLOTS), SLOTS), :] = o.reshape(4, SLOTS, CW)

        def down(i, carry2):
            t0 = c * E + i * G2
            for q in range(G2):
                wait_w2(t0 + q)
            hot = jnp.logical_and(i == 0, me == 0)

            @pl.when(hot)
            def _():
                def hot_down(s, carry3):
                    o = jnp.dot(zh[s], wbuf[slot(t0)], preferred_element_type=F32).astype(BF16)
                    zhot[s] = meta[s].T[:, 13:14] * o.astype(F32)
                    return carry3

                lax.fori_loop(0, 4, hot_down, 0)
                ob[:, HOT_ID * SLOTS:(HOT_ID + 1) * SLOTS, :] = jnp.zeros((4, SLOTS, CW), BF16)

            @pl.when(jnp.logical_not(hot))
            def _():
                cold_down(t0)

            for q in range(1, G2):
                cold_down(t0 + q)

            @pl.when(t0 + N2 < NC * E)
            def _():
                for q in range(G2):
                    start_w2(t0 + N2 + q)
            return carry2

        lax.fori_loop(0, E // G2, down, 0)

        def combine(s):
            r = jnp.dot(cm[s], ob[s], preferred_element_type=F32)
            return (r[0:T] + r[T:2 * T]) + r[2 * T:3 * T] + zhot[s]

        p = c % 2
        d_cp = remote(sdiag.at[p], rdiag.at[c], dg_send.at[p], dg_recv.at[c], sib)
        s_cp = remote(ssib.at[p], rsib.at[c], sb_send.at[p], sb_recv.at[c], sib)
        x_cp = remote(scpt.at[c], rcpt.at[c], cp_send.at[c], cp_recv.at[c], cpt)

        @pl.when(c >= 2)
        def _():
            d_cp.wait_send()
            s_cp.wait_send()

        sdiag[p] = combine(3)
        d_cp.start()
        ssib[p] = combine(1)
        s_cp.start()
        scpt[c] = combine(2)
        own[c] = combine(0)
        d_cp.wait_recv()
        scpt[c] = scpt[c] + rdiag[c]
        x_cp.start()
        return carry

    zhot[...] = jnp.zeros_like(zhot)
    lax.fori_loop(0, NC, chunk, 0)

    for c in range(NC):
        cs = slice(c * CW, c * CW + CW)
        remote(ssib.at[0], rsib.at[c], sb_send.at[0], sb_recv.at[c], sib).wait_recv()
        remote(scpt.at[c], rcpt.at[c], cp_send.at[c], cp_recv.at[c], cpt).wait_recv()
        y_ref[:, cs] = (own[c] + rsib[c] + rcpt[c]).astype(BF16)

    m_sib.wait_send()
    m_cpt.wait_send()
    m_fwd.wait_send()
    for i in range(2):
        u_sib[i].wait_send()
    for k in range(NU):
        u_cpt(k).wait_send()
        u_fwd(k).wait_send()
    for p in range(2):
        remote(sdiag.at[p], rdiag.at[p], dg_send.at[p], dg_recv.at[p], sib).wait_send()
        remote(ssib.at[p], rsib.at[p], sb_send.at[p], sb_recv.at[p], sib).wait_send()
    for c in range(NC):
        remote(scpt.at[c], rcpt.at[c], cp_send.at[c], cp_recv.at[c], cpt).wait_send()


def _moe(q, k, v, x, wo, ln2, meta, w1, w3, w2, KC):
    NH, T, DH = q.shape
    D = x.shape[1]
    E, _, FF = w1.shape
    CW = 512
    NC = D // CW
    R = E * SLOTS
    dma = pltpu.SemaphoreType.DMA
    cos, sin = _tables(T, DH)
    vm = pl.BlockSpec(memory_space=pltpu.VMEM)
    any_spec = pl.BlockSpec(memory_space=pl.ANY)
    part = pltpu.VMEM((NC, T, CW), F32)
    flops = 6 * D * FF * (E * 4 * SLOTS + T)
    return pl.pallas_call(
        functools.partial(_moe_kernel, KC, CW),
        out_shape=jax.ShapeDtypeStruct((T, D), BF16),
        in_specs=[any_spec] * 5 + [vm] * 3 + [any_spec] * 4,
        out_specs=pl.BlockSpec(memory_space=pltpu.VMEM),
        scratch_shapes=[
            pltpu.VMEM((4, T, D), BF16),
            pltpu.VMEM((4, 16, T), F32),
            pltpu.VMEM((E, 4 * SLOTS, D), BF16),
            pltpu.VMEM((4 * SLOTS, FF), BF16),
            pltpu.VMEM((4, T, FF), BF16),
            pltpu.VMEM((NW, D, FF), BF16),
            pltpu.VMEM((4, R, CW), BF16),
            pltpu.VMEM((4, 3 * T, R), BF16),
            pltpu.VMEM((4, R, T), BF16),
            pltpu.VMEM((4, T, CW), F32),
            pltpu.VMEM((2, T, CW), F32),
            pltpu.VMEM((2, T, CW), F32),
            part, part, part, part, part,
            dma((5,)), dma((NH,)), dma((NH,)), dma((NH,)), dma((NW,)), dma((N2,)),
            dma((3,)), dma((3,)),
            dma((NU,)), dma((NU,)), dma((NU,)), dma((NU,)),
            dma((2,)), dma((2,)),
            dma((2,)), dma((NC,)), dma((2,)), dma((NC,)), dma((NC,)), dma((NC,)),
        ],
        compiler_params=pltpu.CompilerParams(
            collective_id=0, has_side_effects=True, vmem_limit_bytes=67000000),
        cost_estimate=pl.CostEstimate(flops=flops, bytes_accessed=6 * E * D * FF, transcendentals=0),
        name='moe',
    )(q, k, v, x, wo.reshape(D, D), jnp.asarray(cos), jnp.asarray(sin), ln2.reshape(1, D), meta, w1, w3, w2)


def solution(mesh):
    def local(x, idx, g, hot_tok, hot_g, ln1, wq, wk, wv, wo, ln2, w1, w3, w2):
        n_exp = w1.shape[0] * mesh.shape['expert']
        meta = _meta(idx, g, hot_tok, hot_g, n_exp)
        a = _rms(x, ln1)
        q = jnp.einsum('td,dhk->htk', a, wq, preferred_element_type=F32)
        k = jnp.einsum('td,dhk->htk', a, wk, preferred_element_type=F32)
        v = jnp.einsum('td,dhk->htk', a, wv, preferred_element_type=F32).astype(BF16)
        return _moe(q, k, v, x, wo, ln2, meta, w1, w3, w2, idx.shape[1])

    tk = ('data', 'expert')
    rep3 = P(None, None, None)
    exp3 = P('expert', None, None)
    return jax.shard_map(
        local, mesh=mesh,
        in_specs=(P(tk, None), P(tk, None), P(tk, None), P(tk), P(tk), P(None),
                  rep3, rep3, rep3, rep3, P(None), exp3, exp3, exp3),
        out_specs=P(tk, None), check_vma=False)
```

time: 210 us -> 183 us (0.87)
  local copies, waits for them, and re-layouts: 29.9 us -> 4.22 us
  Pallas kernels: 149 us -> 152 us
  other arithmetic: 7.22 us -> 4.58 us
    unnamed x21 -> x5, local copies, waits for them, and re-layouts: 28 us -> 2.31 us
    unnamed x2 -> x0, matrix products: 11.7 us -> none
    dot_general x3, matrix products: 11 us -> 21.4 us  [the longest x1 7.17 us: local(): jnp.einsum('td,dhk->htk', a, wv, preferred_element_type=F32).astype(BF16)]
    sub x1 -> x0, other arithmetic: 3.12 us -> none  [_attention(): p = jax.nn.softmax(jnp.where(mask[None], s, -jnp.inf), axis=-1).astype(BF16)]
    pallas_call x1, Pallas kernels: 149 us -> 152 us  [_moe(): pl.pallas_call(functools.partial(_moe_kernel, KC, CW), out_shape=jax.Shap...]
where the time goes in v2:
time: 183 us; the launch traced here: 182 us
  Pallas kernels  152 us (83%)
  matrix products  21.6 us (12%)
  other arithmetic  4.58 us (3%)
  local copies, waits for them, and re-layouts  4.22 us (2%)
    pallas_call x1, Pallas kernels, _moe(): pl.pallas_call(functools.partial(_moe_kernel, KC, CW), out_shape=jax.Shap...  152 us
    dot_general x1, matrix products, local(): jnp.einsum('td,dhk->htk', a, wv, preferred_element_type=F32).astype(BF16)  7.17 us
    dot_general x1, matrix products, local(): q = jnp.einsum('td,dhk->htk', a, wq, preferred_element_type=F32)  7.13 us
    dot_general x1, matrix products, local(): k = jnp.einsum('td,dhk->htk', a, wk, preferred_element_type=F32)  7.06 us

profile of v2, /device:TPU:0, one launch (start us, length us, event | category | flops | bytes accessed | tf_op | source)
XLA Modules:
  0.0 182.3 jit_solution(1280461017699380849)
XLA Ops:
  0.0 0.8 select_reduce_fusion.1
  0.8 1.5 fusion.6
  2.4 0.7 fusion.22
  3.1 0.2 fusion.24
  3.4 0.8 select_reduce_fusion
  4.1 0.7 add_bitcast_fusion
  4.8 1.9 %concatenate.3.meta_hbm = f32[16,256]{1,0:T(8,128)} concatenate(f32[5,256]{1,0:T(8,128)S(1)} %add_bitcast_fusion, f32[3,256]{1,0:T(4,128)S(1)} %broadcast_in_dim.52, f32[5,256]{1,0:T(8,128)} %bitcast.20, f32[1,256]{1,0:T(1,128)S(1)} %bitcast.21, f32[2,256]{1,0:T(2,128)S(1)} %broadcast_in_dim.56), dimensions={0} | concatenate | bytes 32768 | tf_op jit(solution)/shard_map/concatenate | solution.py:43
  6.7 0.0 copy-start
  6.8 0.0 copy-start.1
  6.8 7.2 %fusion.18.v_hbm = bf16[16,256,128]{2,1,0:T(8,128)(2,1)} fusion(bf16[2048,16,128]{2,1,0:T(8,128)(2,1)} %param.24, bf16[256,2048]{1,0:T(8,128)(2,1)} %x_hbm.1, f32[2048]{0:T(1024)} %param.21, f32[256]{0:T(256)S(1)} %add_rsqrt_fusion), kind=kOutput, calls=%fused_computation.14 | convolution fusion | flops 2150105088 | bytes 10494976 | tf_op jit(solution)/shard_map/td,dhk->htk/dot_general | solution.py:469
  13.9 0.0 copy-done
  13.9 0.0 copy-done.1
  13.9 7.1 %fusion.12.k_hbm = f32[16,256,128]{2,1,0:T(8,128)} fusion(bf16[2048,16,128]{2,1,0:T(8,128)(2,1)} %param.23, bf16[256,2048]{1,0:T(8,128)(2,1)S(1)} %copy-done, f32[2048]{0:T(1024)S(1)} %copy-done.1, f32[256]{0:T(256)S(1)} %add_rsqrt_fusion), kind=kOutput, calls=%fused_computation.12 | convolution fusion | flops 2149580800 | bytes 11543552 | tf_op jit(solution)/shard_map/td,dhk->htk/dot_general | solution.py:468
  21.0 7.1 %fusion.9.q_hbm = f32[16,256,128]{2,1,0:T(8,128)} fusion(bf16[2048,16,128]{2,1,0:T(8,128)(2,1)} %param.22, bf16[256,2048]{1,0:T(8,128)(2,1)S(1)} %copy-done, f32[2048]{0:T(1024)S(1)} %copy-done.1, f32[256]{0:T(256)S(1)} %add_rsqrt_fusion), kind=kOutput, calls=%fused_computation.11 | convolution fusion | flops 2149580800 | bytes 11543552 | tf_op jit(solution)/shard_map/td,dhk->htk/dot_general | solution.py:467
  28.1 151.9 %moe.1 = bf16[256,2048]{1,0:T(8,128)(2,1)} custom-call(f32[16,256,128]{2,1,0:T(8,128)} %fusion.9.q_hbm, f32[16,256,128]{2,1,0:T(8,128)} %fusion.12.k_hbm, bf16[16,256,128]{2,1,0:T(8,128)(2,1)} %fusion.18.v_hbm, bf16[256,2048]{1,0:T(8,128)(2,1)} %x_hbm.1, bf16[2048,2048]{1,0:T(8,128)(2,1)} %bitcast.18, f32[256,128]{1,0:T(8,128)} %constant.26.clone.cos_ref, ...), custom_call_target="tpu_custom_call" | custom-call | flops 39862665216 | bytes 276824064 | tf_op jit(solution)/shard_map/moe/pallas_call | solution.py:430
  180.0 2.3 %copy.40 = bf16[256,2048]{1,0:T(8,128)(2,1)} copy(bf16[256,2048]{1,0:T(8,128)(2,1)} %moe.1) | data formatting | bytes 2097152
  (4 shorter events, 0.0 us)
Async XLA Ops:
  6.7 7.2 %copy-start = (bf16[256,2048]{1,0:T(8,128)(2,1)S(1)}, bf16[256,2048]{1,0:T(8,128)(2,1)}, u32[]{:S(2)}) copy-start(bf16[256,2048]{1,0:T(8,128)(2,1)} %x_hbm.1) | copy-start | bytes 3145732
  6.8 7.2 %copy-start.1 = (f32[2048]{0:T(1024)S(1)}, f32[2048]{0:T(1024)}, u32[]{:S(2)}) copy-start(f32[2048]{0:T(1024)} %param.21) | copy-start | bytes 24580

commit v3 on v2

--- a/solution.py
+++ b/solution.py
@@ -17,11 +17,6 @@
 MESH = pl.DeviceIdType.MESH
 
 
-def _rms(v, w):
-    v = v.astype(F32)
-    return (v * lax.rsqrt(jnp.mean(v * v, axis=-1, keepdims=True) + EPS) * w).astype(BF16)
-
-
 def _tables(n_tok, dh):
     half = dh // 2
     freq = np.float32(ROPE_BASE) ** (-np.arange(half, dtype=np.float32) / np.float32(half))
@@ -31,17 +26,87 @@
     return np.concatenate([cos, cos], axis=1), np.concatenate([-sin, sin], axis=1)
 
 
-def _meta(idx, g, hot_tok, hot_g, n_exp):
-    T, KC = idx.shape
-    eq = idx[:, :, None] == jnp.arange(n_exp)[None, None, :]
-    a = jnp.any(eq, axis=1).astype(BF16)
-    low = jnp.tril(jnp.ones((T, T), BF16), -1)
-    before = jnp.dot(low, a, preferred_element_type=F32)
-    rank = jnp.sum(jnp.where(eq, before[:, None, :], 0.0), axis=-1)
-    slot = idx.astype(F32) * SLOTS + rank
-    hg = jnp.sum(jnp.where(hot_tok[:, None] == jnp.arange(T)[None, :], hot_g[:, None], 0.0), axis=0)
-    return jnp.concatenate(
-        [slot.T, jnp.full((8 - KC, T), -1.0, F32), g.T, hg[None], jnp.zeros((7 - KC, T), F32)], axis=0)
+def _qkv_kernel(n_exp, x_ref, ln1_ref, cos_ref, sin_ref, idx_ref, g_ref, tok_ref, hg_ref, wv, wk, wq,
+                v_ref, k_ref, q_ref, meta_ref, wb, acc, ab, sem):
+    T, D = x_ref.shape
+    NH, _, DH = q_ref.shape
+    NB, KB = wb.shape[1], wb.shape[2]
+    ws = (wv, wk, wq)
+
+    def copy(i, b):
+        return pltpu.make_async_copy(ws[i].at[pl.ds(b * KB, KB)], wb.at[i, b], sem.at[i, b])
+
+    for i in range(3):
+        for b in range(NB):
+            copy(i, b).start()
+
+    ss = jnp.zeros((T, 1), F32)
+    for c in range(0, D, 512):
+        xc = x_ref[:, c:c + 512].astype(F32)
+        ss = ss + jnp.sum(xc * xc, axis=1, keepdims=True)
+    inv = lax.rsqrt(ss * (1.0 / D) + EPS)
+    for c in range(0, D, 512):
+        ab[:, c:c + 512] = (x_ref[:, c:c + 512].astype(F32) * inv * ln1_ref[0:1, c:c + 512]).astype(BF16)
+
+    KC = idx_ref.shape[0]
+    e_iota = lax.broadcasted_iota(jnp.int32, (n_exp, T), 0)
+    hits = [e_iota == idx_ref[j:j + 1, :] for j in range(KC)]
+    member = hits[0]
+    for h in hits[1:]:
+        member = jnp.logical_or(member, h)
+    earlier = lax.broadcasted_iota(jnp.int32, (T, T), 0) < lax.broadcasted_iota(jnp.int32, (T, T), 1)
+    before = jnp.dot(jnp.where(member, 1.0, 0.0).astype(BF16), jnp.where(earlier, 1.0, 0.0).astype(BF16),
+                     preferred_element_type=F32)
+    meta_ref[...] = jnp.full((16, T), -1.0, F32)
+    for j in range(KC):
+        rank = jnp.sum(jnp.where(hits[j], before, 0.0), axis=0, keepdims=True)
+        meta_ref[j:j + 1, :] = idx_ref[j:j + 1, :].astype(F32) * SLOTS + rank
+        meta_ref[8 + j:9 + j, :] = g_ref[j:j + 1, :]
+    tok = jnp.broadcast_to(tok_ref[...].astype(F32), (8, T)).T[:, 0:1]
+    hg = jnp.broadcast_to(hg_ref[...], (8, T)).T[:, 0:1]
+    t_iota = lax.broadcasted_iota(jnp.int32, (T, T), 1).astype(F32)
+    meta_ref[13:14, :] = jnp.sum(jnp.where(tok == t_iota, hg, 0.0), axis=0, keepdims=True)
+
+    for i, out in enumerate((v_ref, k_ref, q_ref)):
+        for b in range(NB):
+            copy(i, b).wait()
+            part = jnp.dot(ab[:, b * KB:(b + 1) * KB], wb[i, b].reshape(KB, D), preferred_element_type=F32)
+            if b < NB - 1:
+                acc[...] = part if b == 0 else acc[...] + part
+                continue
+            for h in range(NH):
+                t = part[:, h * DH:(h + 1) * DH]
+                if NB > 1:
+                    t = t + acc[:, h * DH:(h + 1) * DH]
+                if i > 0:
+                    t = t * cos_ref[...] + pltpu.roll(t, DH // 2, 1) * sin_ref[...]
+                out[h] = t.astype(BF16)
+
+
+def _qkv(x, ln1, wq, wk, wv, idx, g, hot_tok, hot_g, n_exp):
+    T, D = x.shape
+    _, NH, DH = wq.shape
+    NB = 2
+    cos, sin = _tables(T, DH)
+    vm = pl.BlockSpec(memory_space=pltpu.VMEM)
+    any_spec = pl.BlockSpec(memory_space=pl.ANY)
+    head = jax.ShapeDtypeStruct((NH, T, DH), BF16)
+    return pl.pallas_call(
+        functools.partial(_qkv_kernel, n_exp),
+        out_shape=[head, head, head, jax.ShapeDtypeStruct((16, T), F32)],
+        in_specs=[vm] * 8 + [any_spec] * 3,
+        out_specs=[vm] * 4,
+        scratch_shapes=[
+            pltpu.VMEM((3, NB, D // NB, NH, DH), BF16),
+            pltpu.VMEM((T, D), F32),
+            pltpu.VMEM((T, D), BF16),
+            pltpu.SemaphoreType.DMA((3, NB)),
+        ],
+        compiler_params=pltpu.CompilerParams(vmem_limit_bytes=60000000),
+        cost_estimate=pl.CostEstimate(flops=6 * T * D * D, bytes_accessed=6 * D * D, transcendentals=0),
+        name='qkv',
+    )(x, ln1.reshape(1, D), jnp.asarray(cos), jnp.asarray(sin), idx.T, g.T, hot_tok.reshape(1, T),
+      hot_g.reshape(1, T), wv, wk, wq)
 
 
 NU = 4
@@ -50,8 +115,8 @@
 G2 = 4
 
 
-def _moe_kernel(KC, CW, q_hbm, k_hbm, v_hbm, x_hbm, wo, cos_ref, sin_ref, ln2_ref, meta_hbm, w1, w3, w2, y_ref,
-                u_all, meta, xs, zt, zh, wbuf, ob, cm, sel, zhot, sdiag, ssib, scpt, own, rdiag, rsib, rcpt,
+def _moe_kernel(KC, CW, q_hbm, k_hbm, v_hbm, x_hbm, wo, ln2_ref, meta_hbm, w1, w3, w2, y_ref,
+                u_all, meta, xs, zt, zh, wbuf, ob, cm, sel, hgc, zhot, sdiag, ssib, scpt, own, rdiag, rsib, rcpt,
                 in_sem, q_sem, k_sem, v_sem, wsem, w2sem, um_send, um_recv, uc_send, uc_recv, uf_send, uf_recv,
                 us_send, us_recv, dg_send, dg_recv, sb_send, sb_recv, cp_send, cp_recv):
     me = lax.axis_index('expert')
@@ -90,17 +155,15 @@
 
     HB = CW // DH
 
-    def head_copy(src, dst, sem, h):
-        c, lane = h // HB, (h % HB) * DH
-        return pltpu.make_async_copy(src.at[h], dst.at[c, pl.ds(0, T), pl.ds(lane, DH)], sem.at[h])
-
-    def head_wait(src, dst, sem, c, j):
-        pltpu.make_async_copy(src.at[0], dst.at[c, pl.ds(0, T), pl.ds(j * DH, DH)], sem.at[c * HB + j]).wait()
+    bufs = ((q_hbm, zh, 0, q_sem), (k_hbm, ob, T, k_sem), (v_hbm, ob, 0, v_sem))
+
+    def head_copy(b, h, c, j):
+        src, dst, r0, sem = bufs[b]
+        return pltpu.make_async_copy(src.at[h], dst.at[c, pl.ds(r0, T), pl.ds(j * DH, DH)], sem.at[c * HB + j])
 
     for h in range(NH):
-        head_copy(q_hbm, own, q_sem, h).start()
-        head_copy(k_hbm, scpt, k_sem, h).start()
-        head_copy(v_hbm, ob, v_sem, h).start()
+        for b in range(3):
+            head_copy(b, h, h // HB, h % HB).start()
     cx = [pltpu.make_async_copy(x_hbm.at[pl.ds(i * HT, HT)], xs.at[2 + i], in_sem.at[i]) for i in range(2)]
     cwo = [pltpu.make_async_copy(wo.at[:, pl.ds(i * D // 2, D // 2)], wbuf.at[2 + i, :, pl.ds(0, D // 2)],
                                  in_sem.at[2 + i]) for i in range(2)]
@@ -137,33 +200,23 @@
     def attend(half):
         r0 = half * HT
         nk = r0 + HT
-        cos = cos_ref[r0:nk, :]
-        sin = sin_ref[r0:nk, :]
-
-        def rope(t):
-            return (t * cos + pltpu.roll(t, DH // 2, 1) * sin).astype(BF16)
-
         row = lax.broadcasted_iota(jnp.int32, (HT, nk), 0) + r0
         seen = row >= lax.broadcasted_iota(jnp.int32, (HT, nk), 1)
 
         def heads(c, carry):
+            if half == 0:
+                for j in range(HB):
+                    for b in range(3):
+                        head_copy(b, 0, c, j).wait()
+            lanes = [slice(j * DH, (j + 1) * DH) for j in range(HB)]
+            sc = [lax.dot_general(zh[c, r0:nk, ls], ob[c, T:T + nk, ls], (((1,), (1,)), ((), ())),
+                                  preferred_element_type=F32) for ls in lanes]
+            sc = [jnp.where(seen, s * scale, -jnp.inf) for s in sc]
+            ps = [jnp.exp(s - jnp.max(s, axis=1, keepdims=True)) for s in sc]
+            ps = [(p * (1.0 / jnp.sum(p, axis=1, keepdims=True))).astype(BF16) for p in ps]
+            os = [jnp.dot(p, ob[c, 0:nk, ls], preferred_element_type=F32) for p, ls in zip(ps, lanes)]
             for j in range(HB):
-                ls = slice(j * DH, (j + 1) * DH)
-                if half == 0:
-                    head_wait(q_hbm, own, q_sem, c, j)
-                    head_wait(k_hbm, scpt, k_sem, c, j)
-                    head_wait(v_hbm, ob, v_sem, c, j)
-            for j in range(HB):
-                ls = slice(j * DH, (j + 1) * DH)
-                q = rope(own[c, r0:nk, ls])
-                ob[c, T + r0:T + nk, ls] = rope(scpt[c, r0:nk, ls])
-                s = lax.dot_general(q, ob[c, T:T + nk, ls], (((1,), (1,)), ((), ())),
-                                    preferred_element_type=F32) * scale
-                s = jnp.where(seen, s, -jnp.inf)
-                p = jnp.exp(s - jnp.max(s, axis=1, keepdims=True))
-                p = (p * (1.0 / jnp.sum(p, axis=1, keepdims=True))).astype(BF16)
-                o = jnp.dot(p, ob[c, 0:nk, ls], preferred_element_type=F32)
-                xs[half, :, pl.ds(pl.multiple_of(c * CW + j * DH, DH), DH)] = o.astype(BF16)
+                xs[half, :, pl.ds(pl.multiple_of(c * CW + j * DH, DH), DH)] = os[j].astype(BF16)
             return carry
 
         lax.fori_loop(0, NH // HB, heads, 0)
@@ -218,6 +271,7 @@
         r1 = gate - hi.astype(F32)
         mid = r1.astype(BF16)
         lo = (r1 - mid.astype(F32)).astype(BF16)
+        hgc[s] = mc[:, 13:14]
         cm[s, 0:T, :] = hi
         cm[s, T:2 * T, :] = mid
         cm[s, 2 * T:3 * T, :] = lo
@@ -344,7 +398,7 @@
             def _():
                 def hot_down(s, carry3):
                     o = jnp.dot(zh[s], wbuf[slot(t0)], preferred_element_type=F32).astype(BF16)
-                    zhot[s] = meta[s].T[:, 13:14] * o.astype(F32)
+                    zhot[s] = hgc[s] * o.astype(F32)
                     return carry3
 
                 lax.fori_loop(0, 4, hot_down, 0)
@@ -422,7 +476,6 @@
     NC = D // CW
     R = E * SLOTS
     dma = pltpu.SemaphoreType.DMA
-    cos, sin = _tables(T, DH)
     vm = pl.BlockSpec(memory_space=pltpu.VMEM)
     any_spec = pl.BlockSpec(memory_space=pl.ANY)
     part = pltpu.VMEM((NC, T, CW), F32)
@@ -430,7 +483,7 @@
     return pl.pallas_call(
         functools.partial(_moe_kernel, KC, CW),
         out_shape=jax.ShapeDtypeStruct((T, D), BF16),
-        in_specs=[any_spec] * 5 + [vm] * 3 + [any_spec] * 4,
+        in_specs=[any_spec] * 5 + [vm] + [any_spec] * 4,
         out_specs=pl.BlockSpec(memory_space=pltpu.VMEM),
         scratch_shapes=[
             pltpu.VMEM((4, T, D), BF16),
@@ -442,6 +495,7 @@
             pltpu.VMEM((4, R, CW), BF16),
             pltpu.VMEM((4, 3 * T, R), BF16),
             pltpu.VMEM((4, R, T), BF16),
+            pltpu.VMEM((4, T, 1), F32),
             pltpu.VMEM((4, T, CW), F32),
             pltpu.VMEM((2, T, CW), F32),
             pltpu.VMEM((2, T, CW), F32),
@@ -456,17 +510,13 @@
             collective_id=0, has_side_effects=True, vmem_limit_bytes=67000000),
         cost_estimate=pl.CostEstimate(flops=flops, bytes_accessed=6 * E * D * FF, transcendentals=0),
         name='moe',
-    )(q, k, v, x, wo.reshape(D, D), jnp.asarray(cos), jnp.asarray(sin), ln2.reshape(1, D), meta, w1, w3, w2)
+    )(q, k, v, x, wo.reshape(D, D), ln2.reshape(1, D), meta, w1, w3, w2)
 
 
 def solution(mesh):
     def local(x, idx, g, hot_tok, hot_g, ln1, wq, wk, wv, wo, ln2, w1, w3, w2):
         n_exp = w1.shape[0] * mesh.shape['expert']
-        meta = _meta(idx, g, hot_tok, hot_g, n_exp)
-        a = _rms(x, ln1)
-        q = jnp.einsum('td,dhk->htk', a, wq, preferred_element_type=F32)
-        k = jnp.einsum('td,dhk->htk', a, wk, preferred_element_type=F32)
-        v = jnp.einsum('td,dhk->htk', a, wv, preferred_element_type=F32).astype(BF16)
+        v, k, q, meta = _qkv(x, ln1, wq, wk, wv, idx, g, hot_tok, hot_g, n_exp)
         return _moe(q, k, v, x, wo, ln2, meta, w1, w3, w2, idx.shape[1])
 
     tk = ('data', 'expert')

time: 183 us -> 167 us (0.913)
  matrix products: 21.6 us -> 0 us
  Pallas kernels: 152 us -> 165 us
  other arithmetic: 4.58 us -> 0 us
  local copies, waits for them, and re-layouts: 4.22 us -> 2.3 us
    dot_general x4 -> x0, matrix products: 21.6 us -> none  [the longest x1 7.17 us: local(): jnp.einsum('td,dhk->htk', a, wv, preferred_element_type=F32).astype(BF16)]
    pallas_call x0 -> x1, Pallas kernels: none -> 15.6 us  [_qkv(): pl.pallas_call(functools.partial(_qkv_kernel, n_exp), out_shape=[head, he...]
    reduce_sum x3 -> x0, other arithmetic: 3.12 us -> none  [the longest x1 1.51 us: _rms(): jnp.mean(v * v, axis=-1, keepdims=True) + EPS]
    pallas_call x1, Pallas kernels: 152 us -> 149 us  [_moe(): pl.pallas_call(functools.partial(_moe_kernel, KC, CW), out_shape=jax.Shap...]
    concatenate x1 -> x0, local copies, waits for them, and re-layouts: 1.91 us -> none  [_meta(): jnp.concatenate([slot.T, jnp.full((8 - KC, T), -1.0, F32), g.T, hg[None],...]
where the time goes in v3:
time: 167 us
  Pallas kernels  165 us (99%)
  local copies, waits for them, and re-layouts  2.3 us (1%)
    pallas_call x1, Pallas kernels, _moe(): pl.pallas_call(functools.partial(_moe_kernel, KC, CW), out_shape=jax.Shap...  149 us
    pallas_call x1, Pallas kernels, _qkv(): pl.pallas_call(functools.partial(_qkv_kernel, n_exp), out_shape=[head, he...  15.6 us

profile of v3, /device:TPU:0, one launch (start us, length us, event | category | flops | bytes accessed | tf_op | source)
XLA Modules:
  0.0 167.2 jit_solution(12600095963789449421)
XLA Ops:
  0.0 15.6 %qkv.1 = (bf16[16,256,128]{2,1,0:T(8,128)(2,1)}, bf16[16,256,128]{2,1,0:T(8,128)(2,1)}, bf16[16,256,128]{2,1,0:T(8,128)(2,1)}, f32[16,256]{1,0:T(8,128)}) custom-call(bf16[256,2048]{1,0:T(8,128)(2,1)} %x_hbm.1, f32[1,2048]{1,0:T(1,128)} %bitcast.8, f32[256,128]{1,0:T(8,128)} %constant.4.clone.cos_ref, f32[256,128]{1,0:T(8,128)} %constant.5.clone.sin_ref, ...), custom_call_target="tpu_custom_call" | custom-call | flops 6442450944 | bytes 25165824 | tf_op jit(solution)/shard_map/qkv/pallas_call | solution.py:94
  15.6 149.3 %moe.1 = bf16[256,2048]{1,0:T(8,128)(2,1)} custom-call(bf16[16,256,128]{2,1,0:T(8,128)(2,1)} %get-tuple-element.9.q_hbm, bf16[16,256,128]{2,1,0:T(8,128)(2,1)} %get-tuple-element.10.k_hbm, bf16[16,256,128]{2,1,0:T(8,128)(2,1)} %get-tuple-element.11.v_hbm, bf16[256,2048]{1,0:T(8,128)(2,1)} %x_hbm.1, bf16[2048,2048]{1,0:T(8,128)(2,1)} %bitcast.7, ...), custom_call_target="tpu_custom_call" | custom-call | flops 39862665216 | bytes 276824064 | tf_op jit(solution)/shard_map/moe/pallas_call | solution.py:483
  164.9 2.3 %copy.18 = bf16[256,2048]{1,0:T(8,128)(2,1)} copy(bf16[256,2048]{1,0:T(8,128)(2,1)} %moe.1) | data formatting | bytes 2097152

commit v4 on v3

--- a/solution.py
+++ b/solution.py
@@ -29,8 +29,7 @@
 def _qkv_kernel(n_exp, x_ref, ln1_ref, cos_ref, sin_ref, idx_ref, g_ref, tok_ref, hg_ref, wv, wk, wq,
                 v_ref, k_ref, q_ref, meta_ref, wb, acc, ab, sem):
     T, D = x_ref.shape
-    NH, _, DH = q_ref.shape
-    NB, KB = wb.shape[1], wb.shape[2]
+    _, NB, KB, NH, DH = wb.shape
     ws = (wv, wk, wq)
 
     def copy(i, b):
@@ -80,7 +79,7 @@
                     t = t + acc[:, h * DH:(h + 1) * DH]
                 if i > 0:
                     t = t * cos_ref[...] + pltpu.roll(t, DH // 2, 1) * sin_ref[...]
-                out[h] = t.astype(BF16)
+                out[:, h * DH:(h + 1) * DH] = t.astype(BF16)
 
 
 def _qkv(x, ln1, wq, wk, wv, idx, g, hot_tok, hot_g, n_exp):
@@ -90,7 +89,7 @@
     cos, sin = _tables(T, DH)
     vm = pl.BlockSpec(memory_space=pltpu.VMEM)
     any_spec = pl.BlockSpec(memory_space=pl.ANY)
-    head = jax.ShapeDtypeStruct((NH, T, DH), BF16)
+    head = jax.ShapeDtypeStruct((T, D), BF16)
     return pl.pallas_call(
         functools.partial(_qkv_kernel, n_exp),
         out_shape=[head, head, head, jax.ShapeDtypeStruct((16, T), F32)],
@@ -110,22 +109,24 @@
 
 
 NU = 4
-NW = 4
-N2 = 8
-G2 = 4
-
-
-def _moe_kernel(KC, CW, q_hbm, k_hbm, v_hbm, x_hbm, wo, ln2_ref, meta_hbm, w1, w3, w2, y_ref,
+NW = 5
+G2 = 8
+
+
+def _moe_kernel(KC, CW, DH, q_hbm, k_hbm, v_hbm, x_hbm, wo, ln2_ref, meta_hbm, w1, w3, w2, y_ref,
                 u_all, meta, xs, zt, zh, wbuf, ob, cm, sel, hgc, zhot, sdiag, ssib, scpt, own, rdiag, rsib, rcpt,
-                in_sem, q_sem, k_sem, v_sem, wsem, w2sem, um_send, um_recv, uc_send, uc_recv, uf_send, uf_recv,
+                in_sem, qkv_sem, wsem, w2sem, um_send, um_recv, uc_send, uc_recv, uf_send, uf_recv,
                 us_send, us_recv, dg_send, dg_recv, sb_send, sb_recv, cp_send, cp_recv):
     me = lax.axis_index('expert')
     core = me % 2
     sib = me + 1 - 2 * core
     cpt = (me + 2) % 4
     E, D, FF = w1.shape
-    NH, T, DH = q_hbm.shape
+    T = q_hbm.shape[0]
+    NH = D // DH
     HT = T // 2
+    QW = 512
+    PB = 4
     R = E * SLOTS
     NC = D // CW
     RU = T // NU
@@ -139,9 +140,15 @@
         b = (2 * i + odd) % NW
         pltpu.make_async_copy(src.at[0], wbuf.at[b], wsem.at[b]).wait()
 
+    N2 = NW * PB
+    B2 = (2 * E) % NW
+
+    def w2_slot(t):
+        sl = t % N2
+        return (B2 + sl // PB) % NW, pl.ds(0, FF), pl.ds(pl.multiple_of((sl % PB) * CW, CW), CW)
+
     def w2_dst(t):
-        sl = t % N2
-        return wbuf.at[sl // 2, pl.ds(0, FF), pl.ds(pl.multiple_of((sl % 2) * CW, CW), CW)], w2sem.at[sl]
+        return wbuf.at[w2_slot(t)], w2sem.at[t % N2]
 
     def start_w2(t):
         dst, sem = w2_dst(t)
@@ -153,17 +160,12 @@
         dst, sem = w2_dst(t)
         pltpu.make_async_copy(w2.at[0, :, pl.ds(0, CW)], dst, sem).wait()
 
-    HB = CW // DH
-
-    bufs = ((q_hbm, zh, 0, q_sem), (k_hbm, ob, T, k_sem), (v_hbm, ob, 0, v_sem))
-
-    def head_copy(b, h, c, j):
-        src, dst, r0, sem = bufs[b]
-        return pltpu.make_async_copy(src.at[h], dst.at[c, pl.ds(r0, T), pl.ds(j * DH, DH)], sem.at[c * HB + j])
-
-    for h in range(NH):
-        for b in range(3):
-            head_copy(b, h, h // HB, h % HB).start()
+    HB = QW // DH
+    QB, KB, VB = 4, 6, 8
+    qkv = [[pltpu.make_async_copy(src.at[pl.ds(i * HT, HT)], xs.at[b + i], qkv_sem.at[n, i])
+            for n, (src, b) in enumerate(((q_hbm, QB), (k_hbm, KB), (v_hbm, VB)))] for i in range(2)]
+    for c in qkv[0] + qkv[1]:
+        c.start()
     cx = [pltpu.make_async_copy(x_hbm.at[pl.ds(i * HT, HT)], xs.at[2 + i], in_sem.at[i]) for i in range(2)]
     cwo = [pltpu.make_async_copy(wo.at[:, pl.ds(i * D // 2, D // 2)], wbuf.at[2 + i, :, pl.ds(0, D // 2)],
                                  in_sem.at[2 + i]) for i in range(2)]
@@ -172,6 +174,7 @@
         c.start()
     start_w(0, w1, 0)
     start_w(0, w3, 1)
+    start_w(2, w1, 0)
 
     barrier = pltpu.get_barrier_semaphore()
     for peer in (sib, cpt):
@@ -203,20 +206,23 @@
         row = lax.broadcasted_iota(jnp.int32, (HT, nk), 0) + r0
         seen = row >= lax.broadcasted_iota(jnp.int32, (HT, nk), 1)
 
+        for c in qkv[half]:
+            c.wait()
+
         def heads(c, carry):
-            if half == 0:
-                for j in range(HB):
-                    for b in range(3):
-                        head_copy(b, 0, c, j).wait()
-            lanes = [slice(j * DH, (j + 1) * DH) for j in range(HB)]
-            sc = [lax.dot_general(zh[c, r0:nk, ls], ob[c, T:T + nk, ls], (((1,), (1,)), ((), ())),
+            lanes = [pl.ds(pl.multiple_of(c * QW + j * DH, DH), DH) for j in range(HB)]
+
+            def rows(b, ls):
+                return jnp.concatenate([xs[b + i, :, ls] for i in range(half + 1)], axis=0)
+
+            sc = [lax.dot_general(xs[QB + half, :, ls], rows(KB, ls), (((1,), (1,)), ((), ())),
                                   preferred_element_type=F32) for ls in lanes]
             sc = [jnp.where(seen, s * scale, -jnp.inf) for s in sc]
             ps = [jnp.exp(s - jnp.max(s, axis=1, keepdims=True)) for s in sc]
             ps = [(p * (1.0 / jnp.sum(p, axis=1, keepdims=True))).astype(BF16) for p in ps]
-            os = [jnp.dot(p, ob[c, 0:nk, ls], preferred_element_type=F32) for p, ls in zip(ps, lanes)]
-            for j in range(HB):
-                xs[half, :, pl.ds(pl.multiple_of(c * CW + j * DH, DH), DH)] = os[j].astype(BF16)
+            os = [jnp.dot(p, rows(VB, ls), preferred_element_type=F32) for p, ls in zip(ps, lanes)]
+            for o, ls in zip(os, lanes):
+                xs[half, :, ls] = o.astype(BF16)
             return carry
 
         lax.fori_loop(0, NH // HB, heads, 0)
@@ -225,18 +231,19 @@
             cwo[0].wait()
             cwo[1].wait()
         ss = jnp.zeros((HT, 1), F32)
-        for n in range(NC):
-            cs = slice(n * CW, (n + 1) * CW)
-            wn = (n * CW) // (D // 2)
-            w0 = n * CW - wn * (D // 2)
-            o = jnp.dot(xs[half], wbuf[2 + wn, :, w0:w0 + CW], preferred_element_type=F32)
-            h = (xs[2 + half, :, cs].astype(F32) + o).astype(BF16).astype(F32)
-            zhot[n, 0:HT, :] = h
-            ss = ss + jnp.sum(h * h, axis=1, keepdims=True)
+        for n in range(D // QW):
+            wn = (n * QW) // (D // 2)
+            w0 = n * QW - wn * (D // 2)
+            o = jnp.dot(xs[half], wbuf[2 + wn, :, w0:w0 + QW], preferred_element_type=F32)
+            for z in range(QW // CW):
+                c0 = n * QW + z * CW
+                h = (xs[2 + half, :, c0:c0 + CW].astype(F32) + o[:, z * CW:(z + 1) * CW]).astype(BF16).astype(F32)
+                own[c0 // CW, 0:HT, :] = h
+                ss = ss + jnp.sum(h * h, axis=1, keepdims=True)
         inv = lax.rsqrt(ss * (1.0 / D) + EPS)
         for n in range(NC):
             cs = slice(n * CW, (n + 1) * CW)
-            u_all[0, r0:nk, cs] = (zhot[n, 0:HT, :] * inv * ln2_ref[0:1, cs]).astype(BF16)
+            u_all[0, r0:nk, cs] = (own[n, 0:HT, :] * inv * ln2_ref[0:1, cs]).astype(BF16)
 
     attend(0)
     cm_.wait()
@@ -306,7 +313,7 @@
         for c0, cn in cols:
             a = xs[e]
             h1 = jnp.dot(a, wbuf[b, :, c0:c0 + cn], preferred_element_type=F32)
-            h3 = jnp.dot(a, wbuf[b + 1, :, c0:c0 + cn], preferred_element_type=F32)
+            h3 = jnp.dot(a, wbuf[(b + 1) % NW, :, c0:c0 + cn], preferred_element_type=F32)
             zt[:, c0:c0 + cn] = (jax.nn.silu(h1) * h3).astype(BF16)
         xs[e, :, 0:FF] = zt[...]
 
@@ -333,13 +340,14 @@
     u_fwd(0).start()
 
     def arrive(k, carry):
+        u_fwd(k - 1).wait_recv()
+
+        @pl.when(me == 0)
+        def _():
+            hot_batch(k - 1)
+
         u_cpt(k).wait_recv()
         u_fwd(k).start()
-        u_fwd(k - 1).wait_recv()
-
-        @pl.when(me == 0)
-        def _():
-            hot_batch(k - 1)
         return carry
 
     lax.fori_loop(1, NU, arrive, 0)
@@ -355,8 +363,8 @@
     def _():
         cold_up(HOT_ID, 0)
 
-    start_w(NW // 2, w1, 0)
-    start_w(NW // 2, w3, 1)
+    start_w(2, w3, 1)
+    start_w(3, w1, 0)
 
     def up_step(i, carry):
         e = (i + HOT_ID) % E
@@ -365,56 +373,64 @@
         wait_w(i, w3, 1)
         cold_up(e, b)
 
-        @pl.when(i < E - NW // 2)
-        def _():
-            start_w(i + NW // 2, w1, 0)
-            start_w(i + NW // 2, w3, 1)
-
-        @pl.when(i >= E - NW // 2)
-        def _():
-            for q in range(4):
-                start_w2((i - (E - NW // 2)) * 4 + q)
+        @pl.when(i < E - 2)
+        def _():
+            start_w(i + 2, w3, 1)
+
+        @pl.when(i < E - 3)
+        def _():
+            start_w(i + 3, w1, 0)
+
+        @pl.when(i >= E - 3)
+        def _():
+            n0 = (i - (E - 3)) * 2 * PB
+            for q in range(PB):
+                start_w2(n0 - PB + q + PB * ((E - 1 - i) // 2))
+
+        @pl.when(i >= E - 2)
+        def _():
+            n0 = (i - (E - 3)) * 2 * PB
+            for q in range(PB):
+                start_w2(n0 + q)
         return carry
 
     lax.fori_loop(1, E, up_step, 0)
 
     def chunk(c, carry):
-        def slot(t):
-            sl = t % N2
-            return (sl // 2, pl.ds(0, FF), pl.ds(pl.multiple_of((sl % 2) * CW, CW), CW))
-
         def cold_down(t):
             e = (t % E + HOT_ID) % E
-            o = jnp.dot(xs[e, :, 0:FF], wbuf[slot(t)], preferred_element_type=F32).astype(BF16)
+            o = jnp.dot(xs[e, :, 0:FF], wbuf[w2_slot(t)], preferred_element_type=F32).astype(BF16)
             ob[:, pl.ds(pl.multiple_of(e * SLOTS, SLOTS), SLOTS), :] = o.reshape(4, SLOTS, CW)
+
+        wait_w2(c * E)
+
+        @pl.when(me == 0)
+        def _():
+            def hot_down(s, carry2):
+                z = zh[pl.ds(2 * s, 2)].reshape(2 * T, FF)
+                o = jnp.dot(z, wbuf[w2_slot(c * E)], preferred_element_type=F32).astype(BF16)
+                for q in range(2):
+                    zhot[2 * s + q] = hgc[2 * s + q] * o[q * T:(q + 1) * T].astype(F32)
+                return carry2
+
+            lax.fori_loop(0, 2, hot_down, 0)
 
         def down(i, carry2):
             t0 = c * E + i * G2
+
+            @pl.when(i > 0)
+            def _():
+                wait_w2(t0)
+
+            for q in range(1, G2):
+                wait_w2(t0 + q)
             for q in range(G2):
-                wait_w2(t0 + q)
-            hot = jnp.logical_and(i == 0, me == 0)
-
-            @pl.when(hot)
-            def _():
-                def hot_down(s, carry3):
-                    o = jnp.dot(zh[s], wbuf[slot(t0)], preferred_element_type=F32).astype(BF16)
-                    zhot[s] = hgc[s] * o.astype(F32)
-                    return carry3
-
-                lax.fori_loop(0, 4, hot_down, 0)
-                ob[:, HOT_ID * SLOTS:(HOT_ID + 1) * SLOTS, :] = jnp.zeros((4, SLOTS, CW), BF16)
-
-            @pl.when(jnp.logical_not(hot))
-            def _():
-                cold_down(t0)
-
-            for q in range(1, G2):
                 cold_down(t0 + q)
-
-            @pl.when(t0 + N2 < NC * E)
-            def _():
-                for q in range(G2):
-                    start_w2(t0 + N2 + q)
+            for p in range(0, G2, PB):
+                @pl.when(t0 + N2 + p < NC * E)
+                def _():
+                    for q in range(PB):
+                        start_w2(t0 + N2 + p + q)
             return carry2
 
         lax.fori_loop(0, E // G2, down, 0)
@@ -468,11 +484,10 @@
         remote(scpt.at[c], rcpt.at[c], cp_send.at[c], cp_recv.at[c], cpt).wait_send()
 
 
-def _moe(q, k, v, x, wo, ln2, meta, w1, w3, w2, KC):
-    NH, T, DH = q.shape
-    D = x.shape[1]
+def _moe(q, k, v, x, wo, ln2, meta, w1, w3, w2, KC, DH):
+    T, D = x.shape
     E, _, FF = w1.shape
-    CW = 512
+    CW = 256
     NC = D // CW
     R = E * SLOTS
     dma = pltpu.SemaphoreType.DMA
@@ -481,7 +496,7 @@
     part = pltpu.VMEM((NC, T, CW), F32)
     flops = 6 * D * FF * (E * 4 * SLOTS + T)
     return pl.pallas_call(
-        functools.partial(_moe_kernel, KC, CW),
+        functools.partial(_moe_kernel, KC, CW, DH),
         out_shape=jax.ShapeDtypeStruct((T, D), BF16),
         in_specs=[any_spec] * 5 + [vm] + [any_spec] * 4,
         out_specs=pl.BlockSpec(memory_space=pltpu.VMEM),
@@ -500,7 +515,7 @@
             pltpu.VMEM((2, T, CW), F32),
             pltpu.VMEM((2, T, CW), F32),
             part, part, part, part, part,
-            dma((5,)), dma((NH,)), dma((NH,)), dma((NH,)), dma((NW,)), dma((N2,)),
+            dma((5,)), dma((3, 2)), dma((NW,)), dma((NW * 4,)),
             dma((3,)), dma((3,)),
             dma((NU,)), dma((NU,)), dma((NU,)), dma((NU,)),
             dma((2,)), dma((2,)),
@@ -517,7 +532,7 @@
     def local(x, idx, g, hot_tok, hot_g, ln1, wq, wk, wv, wo, ln2, w1, w3, w2):
         n_exp = w1.shape[0] * mesh.shape['expert']
         v, k, q, meta = _qkv(x, ln1, wq, wk, wv, idx, g, hot_tok, hot_g, n_exp)
-        return _moe(q, k, v, x, wo, ln2, meta, w1, w3, w2, idx.shape[1])
+        return _moe(q, k, v, x, wo, ln2, meta, w1, w3, w2, idx.shape[1], wq.shape[2])
 
     tk = ('data', 'expert')
     rep3 = P(None, None, None)

time: 167 us -> 160 us (0.958)
  Pallas kernels: 165 us -> 157 us
    pallas_call x1, Pallas kernels: 149 us -> 142 us  [_moe(): pl.pallas_call(functools.partial(_moe_kernel, KC, CW, DH), out_shape=jax....]
where the time goes in v4:
time: 160 us
  Pallas kernels  157 us (98%)
  local copies, waits for them, and re-layouts  2.3 us (1%)
    pallas_call x1, Pallas kernels, _moe(): pl.pallas_call(functools.partial(_moe_kernel, KC, CW, DH), out_shape=jax....  142 us
    pallas_call x1, Pallas kernels, _qkv(): pl.pallas_call(functools.partial(_qkv_kernel, n_exp), out_shape=[head, he...  15.7 us

profile of v4, /device:TPU:0, one launch (start us, length us, event | category | flops | bytes accessed | tf_op | source)
XLA Modules:
  0.0 159.6 jit_solution(4431779022605696250)
XLA Ops:
  0.0 15.7 %qkv.1 = (bf16[256,2048]{1,0:T(8,128)(2,1)}, bf16[256,2048]{1,0:T(8,128)(2,1)}, bf16[256,2048]{1,0:T(8,128)(2,1)}, f32[16,256]{1,0:T(8,128)}) custom-call(bf16[256,2048]{1,0:T(8,128)(2,1)} %x_hbm.1, f32[1,2048]{1,0:T(1,128)} %bitcast.8, f32[256,128]{1,0:T(8,128)} %constant.4.clone.cos_ref, f32[256,128]{1,0:T(8,128)} %constant.5.clone.sin_ref, ...), custom_call_target="tpu_custom_call" | custom-call | flops 6442450944 | bytes 25165824 | tf_op jit(solution)/shard_map/qkv/pallas_call | solution.py:93
  15.7 141.6 %moe.1 = bf16[256,2048]{1,0:T(8,128)(2,1)} custom-call(bf16[256,2048]{1,0:T(8,128)(2,1)} %get-tuple-element.9.q_hbm, bf16[256,2048]{1,0:T(8,128)(2,1)} %get-tuple-element.10.k_hbm, bf16[256,2048]{1,0:T(8,128)(2,1)} %get-tuple-element.11.v_hbm, bf16[256,2048]{1,0:T(8,128)(2,1)} %x_hbm.1, bf16[2048,2048]{1,0:T(8,128)(2,1)} %bitcast.7, f32[1,2048]{1,0:T(1,128)} %bitcast.11, ...), custom_call_target="tpu_custom_call" | custom-call | flops 39862665216 | bytes 276824064 | tf_op jit(solution)/shard_map/moe/pallas_call | solution.py:498
  157.3 2.3 %copy.18 = bf16[256,2048]{1,0:T(8,128)(2,1)} copy(bf16[256,2048]{1,0:T(8,128)(2,1)} %moe.1) | data formatting | bytes 2097152

commit v5 on v4

--- a/solution.py
+++ b/solution.py
@@ -172,10 +172,6 @@
     cm_ = pltpu.make_async_copy(meta_hbm, meta.at[0], in_sem.at[4])
     for c in cx + cwo + [cm_]:
         c.start()
-    start_w(0, w1, 0)
-    start_w(0, w3, 1)
-    start_w(2, w1, 0)
-
     barrier = pltpu.get_barrier_semaphore()
     for peer in (sib, cpt):
         pl.semaphore_signal(barrier, inc=1, device_id={'expert': peer}, device_id_type=MESH)
@@ -230,6 +226,9 @@
         if half == 0:
             cwo[0].wait()
             cwo[1].wait()
+            start_w(0, w1, 0)
+            start_w(0, w3, 1)
+            start_w(2, w1, 0)
         ss = jnp.zeros((HT, 1), F32)
         for n in range(D // QW):
             wn = (n * QW) // (D // 2)

time: 160 us -> 158 us (0.988)
    pallas_call x1, Pallas kernels: 142 us -> 140 us  [_moe(): pl.pallas_call(functools.partial(_moe_kernel, KC, CW, DH), out_shape=jax....]
where the time goes in v5:
time: 158 us
  Pallas kernels  156 us (99%)
  local copies, waits for them, and re-layouts  2.3 us (1%)
    pallas_call x1, Pallas kernels, _moe(): pl.pallas_call(functools.partial(_moe_kernel, KC, CW, DH), out_shape=jax....  140 us
    pallas_call x1, Pallas kernels, _qkv(): pl.pallas_call(functools.partial(_qkv_kernel, n_exp), out_shape=[head, he...  15.7 us

profile of v5, /device:TPU:0, one launch (start us, length us, event | category | flops | bytes accessed | tf_op | source)
XLA Modules:
  0.0 157.9 jit_solution(14002249309369023491)
XLA Ops:
  0.0 15.7 %qkv.1 = (bf16[256,2048]{1,0:T(8,128)(2,1)}, bf16[256,2048]{1,0:T(8,128)(2,1)}, bf16[256,2048]{1,0:T(8,128)(2,1)}, f32[16,256]{1,0:T(8,128)}) custom-call(bf16[256,2048]{1,0:T(8,128)(2,1)} %x_hbm.1, f32[1,2048]{1,0:T(1,128)} %bitcast.8, f32[256,128]{1,0:T(8,128)} %constant.4.clone.cos_ref, f32[256,128]{1,0:T(8,128)} %constant.5.clone.sin_ref, ...), custom_call_target="tpu_custom_call" | custom-call | flops 6442450944 | bytes 25165824 | tf_op jit(solution)/shard_map/qkv/pallas_call | solution.py:93
  15.7 139.9 %moe.1 = bf16[256,2048]{1,0:T(8,128)(2,1)} custom-call(bf16[256,2048]{1,0:T(8,128)(2,1)} %get-tuple-element.9.q_hbm, bf16[256,2048]{1,0:T(8,128)(2,1)} %get-tuple-element.10.k_hbm, bf16[256,2048]{1,0:T(8,128)(2,1)} %get-tuple-element.11.v_hbm, bf16[256,2048]{1,0:T(8,128)(2,1)} %x_hbm.1, bf16[2048,2048]{1,0:T(8,128)(2,1)} %bitcast.7, f32[1,2048]{1,0:T(1,128)} %bitcast.11, ...), custom_call_target="tpu_custom_call" | custom-call | flops 39862665216 | bytes 276824064 | tf_op jit(solution)/shard_map/moe/pallas_call | solution.py:497
  155.6 2.3 %copy.18 = bf16[256,2048]{1,0:T(8,128)(2,1)} copy(bf16[256,2048]{1,0:T(8,128)(2,1)} %moe.1) | data formatting | bytes 2097152
